TPU v7x, 128 devices: a whole 4x4x4 slice. The times are simulated.
128 devices in a mesh: rows: 64 (over x_lo, y, z, core), cols: 2 (over x_hi).
Axes of the slice: x: 4 (x_hi: 2, x_lo: 2; x = x_hi * 2 + x_lo), y: 4, z: 4, core: 2. Of those that a mesh axis runs over, the one named last changes fastest.
Arguments:
- design: bfloat16 [131072, 6144], P('rows', 'cols'), may hold values from -0.015625 to 0.015625
- targets: bfloat16 [131072, 128], P('rows'), may hold values from -6 to 6
- col_scale: float32 [6144], P('cols'), may hold values from 0.1 to 1
Outputs:
- solution: float32 [6144, 128], P('cols', 'rows')
- residual: float32 [131072, 128], P('rows')
All inputs are finite; a program needn't handle non-finite values.
Results may differ from a plain program's by a relative error of at most 0.0065.
Values may be sent and summed in bfloat16 or wider, within the bound.
A program may use at most 128 MiB of HBM per device.

v0:
```python
import functools

import jax
import jax.numpy as jnp
from jax import lax
from jax.sharding import Mesh
from jax.sharding import PartitionSpec as P

ITERS = 6
ROWS = ("rows_0", "rows_1", "rows_2", "rows_3")
ROWS_COLS = ("rows_0", "rows_1", "rows_2", "rows_3", "cols")


def split_up(array, dim, size):
    shape = array.shape
    pieces = array.reshape(*shape[:dim], size, shape[dim] // size, *shape[dim + 1 :])
    return jnp.moveaxis(pieces, dim, 0)


def sent_and_summed(array, axis, dim):
    pieces = split_up(array, dim, lax.axis_size(axis))
    arrived = lax.all_to_all(pieces, axis, split_axis=0, concat_axis=0, tiled=True)
    return arrived.sum(axis=0)


def over_axes(array, axes):
    return functools.reduce(lax.psum, axes, array)


def in_order(pieces, dim):
    pieces = jnp.moveaxis(pieces, 0, dim)
    shape = pieces.shape
    return pieces.reshape(*shape[:dim], shape[dim] * shape[dim + 1], *shape[dim + 2 :])


def from_everyone(array, axis):
    copies = jnp.broadcast_to(array, (lax.axis_size(axis), *array.shape))
    return lax.all_to_all(copies, axis, split_axis=0, concat_axis=0, tiled=True)


def gathered_copies(array, axis, dim):
    return in_order(from_everyone(array, axis), dim)


def of_everyone(array, axis):
    return from_everyone(array, axis).astype(jnp.float32).sum(axis=0)


def taken_together(array, axis):
    everything = from_everyone(array, axis)
    return jnp.sum(everything, axis=0)


def local_back(design, vectors):
    return lax.dot_general(
        design, vectors, (((0,), (0,)), ((), ())), preferred_element_type=jnp.float32
    )


def per_device(design, targets, col_scale):
    width = design.shape[1]
    row_count = lax.axis_size(ROWS)
    residual = targets.astype(jnp.float32)
    share = width // row_count
    scale = lax.dynamic_slice_in_dim(col_scale, lax.axis_index(ROWS) * share, share, 0)[:, None]

    def gradient_of(vectors):
        return scale * sent_and_summed(local_back(design, vectors), ROWS, 0)

    def squared(values):
        return over_axes(jnp.sum(values * values, axis=0), ROWS_COLS)

    gradient = gradient_of(targets)
    gamma = squared(gradient)
    solution = jnp.zeros(gradient.shape, jnp.float32)
    direction = gradient
    for step in range(ITERS):
        scaled_dir = (scale * direction).astype(jnp.bfloat16)
        image = of_everyone(
            jnp.dot(
                design, gathered_copies(scaled_dir, ROWS, 0), preferred_element_type=jnp.float32
            ).astype(jnp.bfloat16),
            "cols",
        ).astype(jnp.float32)
        delta = taken_together(jnp.sum(image * image, axis=0), ROWS)
        alpha = gamma / delta
        solution = solution + alpha * direction
        residual = residual - alpha * image
        if step + 1 < ITERS:
            gradient = gradient_of(residual.astype(jnp.bfloat16))
            gamma_new = squared(gradient)
            direction = gradient + gamma_new / gamma * direction
            gamma = gamma_new
    solution_part = lax.all_to_all(solution, ROWS, split_axis=1, concat_axis=0, tiled=True)
    return (solution_part, residual)


def solution(mesh):
    split = Mesh(
        mesh.devices.reshape(2, 4, 4, 2, mesh.shape["cols"]),
        ("rows_0", "rows_1", "rows_2", "rows_3", "cols"),
    )
    in_specs = (P(ROWS, "cols"), P(ROWS, None), P("cols"))
    out_specs = (P("cols", ROWS), P(ROWS, None))
    return jax.shard_map(
        per_device, mesh=split, in_specs=in_specs, out_specs=out_specs, check_vma=False
    )
```

profile of v0, /device:TPU:1, one launch (start us, length us, event | category | flops | bytes accessed | tf_op | source)
XLA Modules:
  0.0 820.6 jit_solution(13330626564013045601)
XLA Ops:
  0.6 9.3 %fusion.13 = f32[3072,128]{1,0:T(8,128)} fusion(bf16[2048,3072]{1,0:T(8,128)(2,1)} %param.3, bf16[2048,128]{1,0:T(8,128)(2,1)} %param.4), kind=kOutput, calls=%fused_computation.58 | convolution fusion | flops 1610612736 | bytes 14680064 | tf_op jit(solution)/shard_map/dot_general | solution.py:55
  9.9 10.9 %all-to-all-start = ((f32[64,48,128]{2,1,0:T(8,128)}), f32[64,48,128]{2,1,0:T(8,128)S(1)}, u32[]{:S(2)}, u32[]{:S(2)}) async-start(f32[64,48,128]{2,1,0:T(8,128)} %bitcast), calls=%async_computation | async-start | bytes 3145728 | tf_op jit(solution)/shard_map/all_to_all | solution.py:22
  21.6 21.7 %all-to-all-done = f32[64,48,128]{2,1,0:T(8,128)S(1)} async-done(((f32[64,48,128]{2,1,0:T(8,128)}), f32[64,48,128]{2,1,0:T(8,128)S(1)}, u32[]{:S(2)}, u32[]{:S(2)}) %all-to-all-start) | async-done | bytes 1572896 | tf_op jit(solution)/shard_map/all_to_all | solution.py:22
  43.6 20.7 %all_to_all.142 = bf16[64,48,128]{2,1,0:T(8,128)(2,1)S(1)} all-to-all(bf16[64,48,128]{2,1,0:T(8,128)(2,1)S(1)} %broadcast_in_dim.72), channel_id=1, replica_groups=mesh['rows_0'=2,'rows_1'=4,'rows_2'=4,'rows_3'=2,'cols'=2] {'rows_0','ro..., dimensions={0} | all-to-all | bytes 1572864 | tf_op jit(solution)/shard_map/all_to_all | solution.py:38
  64.3 8.9 %fusion = bf16[2048,128]{0,1:T(8,128)(2,1)S(1)} fusion(bf16[3072,128]{1,0:T(8,128)(2,1)S(1)} %bitcast.73, bf16[2048,3072]{1,0:T(8,128)(2,1)} %param.3), kind=kOutput, calls=%fused_computation.11 | convolution fusion | flops 1610874880 | bytes 13893632 | tf_op jit(solution)/shard_map/dot_general | solution.py:80
  73.6 18.5 %all_to_all.143 = bf16[2,2048,128]{2,1,0:T(8,128)(2,1)S(1)} all-to-all(bf16[2,2048,128]{2,1,0:T(8,128)(2,1)S(1)} %broadcast_in_dim.73), channel_id=1, replica_groups=mesh['rows_0'=2,'rows_1'=4,'rows_2'=4,'rows_3'=2,'cols'=2] {'cols'}, dimensions={0} | all-to-all | bytes 2097152 | tf_op jit(solution)/shard_map/all_to_all | solution.py:38
  93.2 5.1 all-to-all-start.3
  98.3 4.2 psum.210
  102.5 8.6 %psum.211 = f32[128]{0:T(128)S(1)} all-reduce(f32[128]{0:T(128)S(1)} %psum.210), channel_id=1, replica_groups=mesh['rows_0'=2,'rows_1'=4,'rows_2'=4,'rows_3'=2,'cols'=2] {'rows_1'}, use_global_device_ids=true, to_apply=%region_3.0 | all-reduce | flops 128 | bytes 1024 | tf_op jit(solution)/shard_map/psum | solution.py:27
  111.0 8.4 %psum.212 = f32[128]{0:T(128)S(1)} all-reduce(f32[128]{0:T(128)S(1)} %psum.211), channel_id=1, replica_groups=mesh['rows_0'=2,'rows_1'=4,'rows_2'=4,'rows_3'=2,'cols'=2] {'rows_2'}, use_global_device_ids=true, to_apply=%region_4.0 | all-reduce | flops 128 | bytes 1024 | tf_op jit(solution)/shard_map/psum | solution.py:27
  119.5 7.4 psum.213
  126.9 5.5 psum.214
  132.4 7.6 convolution_bitcast_fusion.4
  141.8 28.0 %all_to_all.144 = f32[64,48,128]{2,1,0:T(8,128)} all-to-all(f32[64,48,128]{2,1,0:T(8,128)S(1)} %bitcast.68), channel_id=1, replica_groups=mesh['rows_0'=2,'rows_1'=4,'rows_2'=4,'rows_3'=2,'cols'=2] {'rows_0','ro..., dimensions={0} | all-to-all | bytes 3145728 | tf_op jit(solution)/shard_map/all_to_all | solution.py:22
  175.2 6.8 psum.216
  182.0 7.1 psum.217
  189.1 8.2 %psum.218 = f32[128]{0:T(128)S(1)} all-reduce(f32[128]{0:T(128)S(1)} %psum.217), channel_id=1, replica_groups=mesh['rows_0'=2,'rows_1'=4,'rows_2'=4,'rows_3'=2,'cols'=2] {'rows_3'}, use_global_device_ids=true, to_apply=%region_15.0 | all-reduce | flops 128 | bytes 1024 | tf_op jit(solution)/shard_map/psum | solution.py:27
  197.3 5.3 psum.219
  202.8 20.0 %all_to_all.145 = bf16[64,48,128]{2,1,0:T(8,128)(2,1)S(1)} all-to-all(bf16[64,48,128]{2,1,0:T(8,128)(2,1)S(1)} %broadcast_in_dim.75), channel_id=1, replica_groups=mesh['rows_0'=2,'rows_1'=4,'rows_2'=4,'rows_3'=2,'cols'=2] {'rows_0','ro..., dimensions={0} | all-to-all | bytes 1572864 | tf_op jit(solution)/shard_map/all_to_all | solution.py:38
  222.8 8.9 %fusion.1 = bf16[2048,128]{0,1:T(8,128)(2,1)S(1)} fusion(bf16[3072,128]{1,0:T(8,128)(2,1)S(1)} %bitcast.74, bf16[2048,3072]{1,0:T(8,128)(2,1)} %param.3), kind=kOutput, calls=%fused_computation.12 | convolution fusion | flops 1610874880 | bytes 13893632 | tf_op jit(solution)/shard_map/dot_general | solution.py:80
  232.1 17.7 %all_to_all.146 = bf16[2,2048,128]{2,1,0:T(8,128)(2,1)S(1)} all-to-all(bf16[2,2048,128]{2,1,0:T(8,128)(2,1)S(1)} %broadcast_in_dim.76), channel_id=1, replica_groups=mesh['rows_0'=2,'rows_1'=4,'rows_2'=4,'rows_3'=2,'cols'=2] {'cols'}, dimensions={0} | all-to-all | bytes 2097152 | tf_op jit(solution)/shard_map/all_to_all | solution.py:38
  250.3 12.8 %all_to_all.147 = f32[64,1,128]{2,1,0:T(1,128)S(1)} all-to-all(f32[64,1,128]{2,1,0:T(1,128)S(1)} %broadcast_in_dim.77), channel_id=1, replica_groups=mesh['rows_0'=2,'rows_1'=4,'rows_2'=4,'rows_3'=2,'cols'=2] {'rows_0','ro..., dimensions={0} | all-to-all | bytes 65536 | tf_op jit(solution)/shard_map/all_to_all | solution.py:38
  264.3 7.5 convolution_bitcast_fusion.3
  274.9 28.5 %all_to_all.148 = f32[64,48,128]{2,1,0:T(8,128)} all-to-all(f32[64,48,128]{2,1,0:T(8,128)} %bitcast.69), channel_id=1, replica_groups=mesh['rows_0'=2,'rows_1'=4,'rows_2'=4,'rows_3'=2,'cols'=2] {'rows_0','ro..., dimensions={0} | all-to-all | bytes 3145728 | tf_op jit(solution)/shard_map/all_to_all | solution.py:22
  308.8 6.8 psum.221
  315.7 7.1 psum.222
  322.8 8.2 %psum.223 = f32[128]{0:T(128)S(1)} all-reduce(f32[128]{0:T(128)S(1)} %psum.222), channel_id=1, replica_groups=mesh['rows_0'=2,'rows_1'=4,'rows_2'=4,'rows_3'=2,'cols'=2] {'rows_3'}, use_global_device_ids=true, to_apply=%region_25.0 | all-reduce | flops 128 | bytes 1024 | tf_op jit(solution)/shard_map/psum | solution.py:27
  331.0 5.3 psum.224
  336.4 20.0 %all_to_all.149 = bf16[64,48,128]{2,1,0:T(8,128)(2,1)S(1)} all-to-all(bf16[64,48,128]{2,1,0:T(8,128)(2,1)S(1)} %broadcast_in_dim.78), channel_id=1, replica_groups=mesh['rows_0'=2,'rows_1'=4,'rows_2'=4,'rows_3'=2,'cols'=2] {'rows_0','ro..., dimensions={0} | all-to-all | bytes 1572864 | tf_op jit(solution)/shard_map/all_to_all | solution.py:38
  356.5 8.9 %fusion.2 = bf16[2048,128]{0,1:T(8,128)(2,1)S(1)} fusion(bf16[3072,128]{1,0:T(8,128)(2,1)S(1)} %bitcast.75, bf16[2048,3072]{1,0:T(8,128)(2,1)} %param.3), kind=kOutput, calls=%fused_computation.13 | convolution fusion | flops 1610874880 | bytes 13893632 | tf_op jit(solution)/shard_map/dot_general | solution.py:80
  365.8 17.7 %all_to_all.150 = bf16[2,2048,128]{2,1,0:T(8,128)(2,1)S(1)} all-to-all(bf16[2,2048,128]{2,1,0:T(8,128)(2,1)S(1)} %broadcast_in_dim.79), channel_id=1, replica_groups=mesh['rows_0'=2,'rows_1'=4,'rows_2'=4,'rows_3'=2,'cols'=2] {'cols'}, dimensions={0} | all-to-all | bytes 2097152 | tf_op jit(solution)/shard_map/all_to_all | solution.py:38
  383.9 12.8 %all_to_all.151 = f32[64,1,128]{2,1,0:T(1,128)S(1)} all-to-all(f32[64,1,128]{2,1,0:T(1,128)S(1)} %broadcast_in_dim.80), channel_id=1, replica_groups=mesh['rows_0'=2,'rows_1'=4,'rows_2'=4,'rows_3'=2,'cols'=2] {'rows_0','ro..., dimensions={0} | all-to-all | bytes 65536 | tf_op jit(solution)/shard_map/all_to_all | solution.py:38
  396.7 7.6 convolution_bitcast_fusion.2
  407.3 28.1 %all_to_all.152 = f32[64,48,128]{2,1,0:T(8,128)} all-to-all(f32[64,48,128]{2,1,0:T(8,128)} %bitcast.70), channel_id=1, replica_groups=mesh['rows_0'=2,'rows_1'=4,'rows_2'=4,'rows_3'=2,'cols'=2] {'rows_0','ro..., dimensions={0} | all-to-all | bytes 3145728 | tf_op jit(solution)/shard_map/all_to_all | solution.py:22
  440.8 6.8 psum.226
  447.6 7.1 psum.227
  454.7 8.2 %psum.228 = f32[128]{0:T(128)S(1)} all-reduce(f32[128]{0:T(128)S(1)} %psum.227), channel_id=1, replica_groups=mesh['rows_0'=2,'rows_1'=4,'rows_2'=4,'rows_3'=2,'cols'=2] {'rows_3'}, use_global_device_ids=true, to_apply=%region_35.0 | all-reduce | flops 128 | bytes 1024 | tf_op jit(solution)/shard_map/psum | solution.py:27
  463.0 5.3 psum.229
  468.4 20.2 %all_to_all.153 = bf16[64,48,128]{2,1,0:T(8,128)(2,1)S(1)} all-to-all(bf16[64,48,128]{2,1,0:T(8,128)(2,1)S(1)} %broadcast_in_dim.81), channel_id=1, replica_groups=mesh['rows_0'=2,'rows_1'=4,'rows_2'=4,'rows_3'=2,'cols'=2] {'rows_0','ro..., dimensions={0} | all-to-all | bytes 1572864 | tf_op jit(solution)/shard_map/all_to_all | solution.py:38
  488.6 8.9 %fusion.3 = bf16[2048,128]{0,1:T(8,128)(2,1)S(1)} fusion(bf16[3072,128]{1,0:T(8,128)(2,1)S(1)} %bitcast.76, bf16[2048,3072]{1,0:T(8,128)(2,1)} %param.3), kind=kOutput, calls=%fused_computation.14 | convolution fusion | flops 1610874880 | bytes 13893632 | tf_op jit(solution)/shard_map/dot_general | solution.py:80
  497.9 17.7 %all_to_all.154 = bf16[2,2048,128]{2,1,0:T(8,128)(2,1)S(1)} all-to-all(bf16[2,2048,128]{2,1,0:T(8,128)(2,1)S(1)} %broadcast_in_dim.82), channel_id=1, replica_groups=mesh['rows_0'=2,'rows_1'=4,'rows_2'=4,'rows_3'=2,'cols'=2] {'cols'}, dimensions={0} | all-to-all | bytes 2097152 | tf_op jit(solution)/shard_map/all_to_all | solution.py:38
  517.0 12.8 %all_to_all.155 = f32[64,1,128]{2,1,0:T(1,128)S(1)} all-to-all(f32[64,1,128]{2,1,0:T(1,128)S(1)} %broadcast_in_dim.83), channel_id=1, replica_groups=mesh['rows_0'=2,'rows_1'=4,'rows_2'=4,'rows_3'=2,'cols'=2] {'rows_0','ro..., dimensions={0} | all-to-all | bytes 65536 | tf_op jit(solution)/shard_map/all_to_all | solution.py:38
  531.2 7.6 convolution_bitcast_fusion.1
  540.7 27.2 %all_to_all.156 = f32[64,48,128]{2,1,0:T(8,128)} all-to-all(f32[64,48,128]{2,1,0:T(8,128)S(1)} %bitcast.71), channel_id=1, replica_groups=mesh['rows_0'=2,'rows_1'=4,'rows_2'=4,'rows_3'=2,'cols'=2] {'rows_0','ro..., dimensions={0} | all-to-all | bytes 3145728 | tf_op jit(solution)/shard_map/all_to_all | solution.py:22
  573.2 6.8 psum.231
  580.1 7.1 psum.232
  587.2 8.2 %psum.233 = f32[128]{0:T(128)S(1)} all-reduce(f32[128]{0:T(128)S(1)} %psum.232), channel_id=1, replica_groups=mesh['rows_0'=2,'rows_1'=4,'rows_2'=4,'rows_3'=2,'cols'=2] {'rows_3'}, use_global_device_ids=true, to_apply=%region_45.0 | all-reduce | flops 128 | bytes 1024 | tf_op jit(solution)/shard_map/psum | solution.py:27
  595.4 5.3 psum.234
  600.9 20.2 %all_to_all.157 = bf16[64,48,128]{2,1,0:T(8,128)(2,1)S(1)} all-to-all(bf16[64,48,128]{2,1,0:T(8,128)(2,1)S(1)} %broadcast_in_dim.84), channel_id=1, replica_groups=mesh['rows_0'=2,'rows_1'=4,'rows_2'=4,'rows_3'=2,'cols'=2] {'rows_0','ro..., dimensions={0} | all-to-all | bytes 1572864 | tf_op jit(solution)/shard_map/all_to_all | solution.py:38
  621.1 8.9 %fusion.4 = bf16[2048,128]{0,1:T(8,128)(2,1)S(1)} fusion(bf16[3072,128]{1,0:T(8,128)(2,1)S(1)} %bitcast.77, bf16[2048,3072]{1,0:T(8,128)(2,1)} %param.3), kind=kOutput, calls=%fused_computation.15 | convolution fusion | flops 1610874880 | bytes 13893632 | tf_op jit(solution)/shard_map/dot_general | solution.py:80
  630.4 17.7 %all_to_all.158 = bf16[2,2048,128]{2,1,0:T(8,128)(2,1)S(1)} all-to-all(bf16[2,2048,128]{2,1,0:T(8,128)(2,1)S(1)} %broadcast_in_dim.85), channel_id=1, replica_groups=mesh['rows_0'=2,'rows_1'=4,'rows_2'=4,'rows_3'=2,'cols'=2] {'cols'}, dimensions={0} | all-to-all | bytes 2097152 | tf_op jit(solution)/shard_map/all_to_all | solution.py:38
  648.5 12.8 %all_to_all.159 = f32[64,1,128]{2,1,0:T(1,128)S(1)} all-to-all(f32[64,1,128]{2,1,0:T(1,128)S(1)} %broadcast_in_dim.86), channel_id=1, replica_groups=mesh['rows_0'=2,'rows_1'=4,'rows_2'=4,'rows_3'=2,'cols'=2] {'rows_0','ro..., dimensions={0} | all-to-all | bytes 65536 | tf_op jit(solution)/shard_map/all_to_all | solution.py:38
  661.4 7.5 convolution_bitcast_fusion
  671.9 28.1 %all_to_all.160 = f32[64,48,128]{2,1,0:T(8,128)} all-to-all(f32[64,48,128]{2,1,0:T(8,128)} %bitcast.72), channel_id=1, replica_groups=mesh['rows_0'=2,'rows_1'=4,'rows_2'=4,'rows_3'=2,'cols'=2] {'rows_0','ro..., dimensions={0} | all-to-all | bytes 3145728 | tf_op jit(solution)/shard_map/all_to_all | solution.py:22
  705.4 6.8 psum.236
  712.3 7.1 psum.237
  719.4 8.2 %psum.238 = f32[128]{0:T(128)S(1)} all-reduce(f32[128]{0:T(128)S(1)} %psum.237), channel_id=1, replica_groups=mesh['rows_0'=2,'rows_1'=4,'rows_2'=4,'rows_3'=2,'cols'=2] {'rows_3'}, use_global_device_ids=true, to_apply=%region_55.0 | all-reduce | flops 128 | bytes 1024 | tf_op jit(solution)/shard_map/psum | solution.py:27
  727.6 5.3 psum.239
  733.1 20.3 %all_to_all.161 = bf16[64,48,128]{2,1,0:T(8,128)(2,1)S(1)} all-to-all(bf16[64,48,128]{2,1,0:T(8,128)(2,1)S(1)} %broadcast_in_dim.87), channel_id=1, replica_groups=mesh['rows_0'=2,'rows_1'=4,'rows_2'=4,'rows_3'=2,'cols'=2] {'rows_0','ro..., dimensions={0} | all-to-all | bytes 1572864 | tf_op jit(solution)/shard_map/all_to_all | solution.py:38
  753.4 8.9 %fusion.5 = bf16[2048,128]{0,1:T(8,128)(2,1)S(1)} fusion(bf16[3072,128]{1,0:T(8,128)(2,1)S(1)} %bitcast.78, bf16[2048,3072]{1,0:T(8,128)(2,1)} %param.3), kind=kOutput, calls=%fused_computation.16 | convolution fusion | flops 1610874880 | bytes 13893632 | tf_op jit(solution)/shard_map/dot_general | solution.py:80
  762.7 17.7 %all_to_all.162 = bf16[2,2048,128]{2,1,0:T(8,128)(2,1)S(1)} all-to-all(bf16[2,2048,128]{2,1,0:T(8,128)(2,1)S(1)} %broadcast_in_dim.88), channel_id=1, replica_groups=mesh['rows_0'=2,'rows_1'=4,'rows_2'=4,'rows_3'=2,'cols'=2] {'cols'}, dimensions={0} | all-to-all | bytes 2097152 | tf_op jit(solution)/shard_map/all_to_all | solution.py:38
  781.4 5.6 all-to-all-start.23
  802.3 9.0 %all-to-all-start.24 = ((f32[48,64,2]{0,2,1:T(2,128)}), f32[48,64,2]{0,2,1:T(2,128)S(1)}, u32[]{:S(2)}, u32[]{:S(2)}) async-start(f32[48,64,2]{0,2,1:T(2,128)} %multiply_add_fusion), calls=%async_computation.24 | async-start | bytes 131072 | tf_op jit(solution)/shard_map/all_to_all | solution.py:94
  813.1 6.4 all-to-all-done.24
  (126 shorter events, 69.4 us)
Async XLA Ops:
  9.9 33.4 %all-to-all-start = ((f32[64,48,128]{2,1,0:T(8,128)}), f32[64,48,128]{2,1,0:T(8,128)S(1)}, u32[]{:S(2)}, u32[]{:S(2)}) async-start(f32[64,48,128]{2,1,0:T(8,128)} %bitcast), calls=%async_computation | async-start | bytes 3145728 | tf_op jit(solution)/shard_map/all_to_all | solution.py:22
  21.6 711.2 %copy-start.2 = (f32[48]{0:T(128)}, f32[48]{0:T(128)S(1)}, u32[]{:S(2)}) copy-start(f32[48]{0:T(128)S(1)} %dynamic_slice.3) | copy-start | bytes 580
  21.6 110.7 %copy-start.1 = (bf16[2048,128]{1,0:T(8,128)(2,1)S(1)}, bf16[2048,128]{1,0:T(8,128)(2,1)}, u32[]{:S(2)}) copy-start(bf16[2048,128]{1,0:T(8,128)(2,1)} %param.4) | copy-start | bytes 1572868
  93.2 39.2 %all-to-all-start.3 = ((f32[64,1,128]{2,1,0:T(1,128)}), f32[64,1,128]{2,1,0:T(1,128)S(1)}, u32[]{:S(2)}, u32[]{:S(2)}) async-start(f32[64,1,128]{2,1,0:T(1,128)} %broadcast_in_dim.74), calls=%async_computation.3 | async-start | bytes 65536 | tf_op jit(solution)/shard_map/all_to_all | solution.py:38
  468.2 63.0 %copy-start.5 = (f32[128]{0:T(128)}, f32[128]{0:T(128)S(1)}, u32[]{:S(2)}) copy-start(f32[128]{0:T(128)S(1)} %div.38) | copy-start | bytes 1540
  515.7 1.0 copy-start
  529.9 10.8 %copy-start.6 = (f32[128]{0:T(128)}, f32[128]{0:T(128)S(1)}, u32[]{:S(2)}) copy-start(f32[128]{0:T(128)S(1)} %div.39) | copy-start | bytes 1540
  600.7 132.2 %copy-start.4 = (f32[128]{0:T(128)}, f32[128]{0:T(128)S(1)}, u32[]{:S(2)}) copy-start(f32[128]{0:T(128)S(1)} %div.40) | copy-start | bytes 1540
  661.4 10.6 %copy-start.3 = (f32[128]{0:T(128)}, f32[128]{0:T(128)S(1)}, u32[]{:S(2)}) copy-start(f32[128]{0:T(128)S(1)} %div.41) | copy-start | bytes 1540
  732.8 47.5 %copy-start.9 = (f32[128]{0:T(128)}, f32[128]{0:T(128)S(1)}, u32[]{:S(2)}) copy-start(f32[128]{0:T(128)S(1)} %psum.239) | copy-start | bytes 1540
  732.9 48.5 %copy-start.7 = (f32[128]{0:T(128)}, f32[128]{0:T(128)S(1)}, u32[]{:S(2)}) copy-start(f32[128]{0:T(128)S(1)} %div.42) | copy-start | bytes 1540
  781.4 16.9 %all-to-all-start.23 = ((f32[64,1,128]{2,1,0:T(1,128)}), f32[64,1,128]{2,1,0:T(1,128)}, u32[]{:S(2)}, u32[]{:S(2)}) async-start(f32[64,1,128]{2,1,0:T(1,128)} %broadcast_in_dim.89), calls=%async_computation.23 | async-start | bytes 65536 | tf_op jit(solution)/shard_map/all_to_all | solution.py:38
  799.7 2.6 copy-start.8
  802.3 17.2 %all-to-all-start.24 = ((f32[48,64,2]{0,2,1:T(2,128)}), f32[48,64,2]{0,2,1:T(2,128)S(1)}, u32[]{:S(2)}, u32[]{:S(2)}) async-start(f32[48,64,2]{0,2,1:T(2,128)} %multiply_add_fusion), calls=%async_computation.24 | async-start | bytes 131072 | tf_op jit(solution)/shard_map/all_to_all | solution.py:94
where the time goes:
time: 831 us; the launch traced here: 821 us
  blocking collectives  609 us (73%)
  matrix products  101 us (12%)
  starting transfers between devices  30.7 us (4%)
  local copies, waits for them, and re-layouts  30.7 us (4%)
  waiting for transfers between devices  28.1 us (3%)
  other arithmetic  19.8 us (2%)
    all_to_all x16, blocking collectives, from_everyone(): return lax.all_to_all(copies, axis, split_axis=0, concat_axis=0, tiled=True)  280 us
    psum x30, blocking collectives, over_axes(): return functools.reduce(lax.psum, axes, array)  190 us
    all_to_all x5, blocking collectives, sent_and_summed(): lax.all_to_all(pieces, axis, split_axis=0, concat_axis=0, tiled=True)  140 us
    dot_general x6, matrix products, per_device(): jnp.dot(design, gathered_copies(scaled_dir, ROWS, 0), preferred_element_t...  53.5 us
    dot_general x6, matrix products, local_back(): lax.dot_general(design, vectors, (((0,), (0,)), ((), ())), preferred_elem...  47 us
    all_to_all x1, waiting for transfers between devices, sent_and_summed(): lax.all_to_all(pieces, axis, split_axis=0, concat_axis=0, tiled=True)  21.7 us
  transfers between devices with their start and end apart: 4, of which 2 were waited for; matrix products, arithmetic and copies ran while one was open for 2% of the time, Pallas kernels for 0%

commit v1 on v0

v1 whole, which is shorter than its diff:
```python
import functools

import jax
import jax.numpy as jnp
from jax import lax
from jax.experimental import pallas as pl
from jax.experimental.pallas import tpu as pltpu
from jax.sharding import PartitionSpec as P

ITERS = 6
NX, NY, NZ, NCORE, NCOL = 2, 4, 4, 2, 2
M_LOC, P_LOC, FITS = 2048, 3072, 128
HALF = FITS // 2
FG = HALF // NZ
LY = P_LOC // NY
CH = 512
NCH = M_LOC // CH
BF, F32 = jnp.bfloat16, jnp.float32
MESH = pl.DeviceIdType.MESH


def wrap_distance(step):
    return min(step, 4 - step)


PLANE = sorted(
    (j for j in range(1, 16)), key=lambda j: -(wrap_distance(j // 4) + wrap_distance(j % 4))
)


def lanes(shape):
    return lax.broadcasted_iota(jnp.int32, shape, len(shape) - 1)


def two_parts(value, first):
    wide = jnp.broadcast_to(value, (value.shape[0], 128))
    high = wide.astype(BF).astype(F32)
    low = (wide - high).astype(BF).astype(F32)
    at = lanes(wide.shape)
    return jnp.where(at == first, high, jnp.where(at == first + 1, low, 0.0))


def kernel(a_hbm, t_ref, s_ref, xo, ro,
           a, q, scal, stile, hacc, hb, hd, hs, dpart, ddp, dlt, rsh, rsd, xs, xr,
           ps, pr, imdp, imdf, res, imt, gv, dv, xv, gam, alf, bet, xpk, fin, fir, fall, fsend,
           a_sem, ex_s, ex_r, d2h_s, d2h_r, d2d_s, d2d_r, rsh_s, rsh_r, rsd_s, rsd_r,
           x_s, x_r, q_s, q_r, sc_s, sc_r, qf_s, qf_r, st_s, st_r, f_s, f_r, g_s, g_r, o_s, o_r):
    r = lax.axis_index("rows")
    col = lax.axis_index("cols")
    core = lax.rem(r, 2)
    chip = r // 2
    z = lax.rem(chip, 4)
    y = lax.rem(chip // 4, 4)
    xl = chip // 16

    def dev(xl_, y_, z_, core_, col_):
        return (((xl_ * 4 + y_) * 4 + z_) * 2 + core_, col_)

    def around(j):
        return lax.rem(y + j // 4, 4), lax.rem(z + j % 4, 4)

    partner = dev(xl, y, z, 1 - core, col)
    across = dev(xl, y, z, core, 1 - col)
    beside = dev(1 - xl, y, z, core, col)

    def remote(src, dst, ss, rs, device):
        return pltpu.make_async_remote_copy(
            src_ref=src, dst_ref=dst, send_sem=ss, recv_sem=rs, device_id=device, device_id_type=MESH)

    for i in range(NCH):
        pltpu.make_async_copy(a_hbm.at[pl.ds(i * CH, CH), :], a.at[pl.ds(i * CH, CH), :], a_sem.at[i]).start()
    barrier = pltpu.get_barrier_semaphore()
    me = r * 2 + col

    def greet(j, carry):
        other = lax.rem(me + j, 128)
        pl.semaphore_signal(barrier, 1, device_id=(other // 2, lax.rem(other, 2)), device_id_type=MESH)
        return carry

    lax.fori_loop(1, 128, greet, 0)
    gv[...] = jnp.zeros(gv.shape, F32)
    dv[...] = jnp.zeros(dv.shape, F32)
    xv[...] = jnp.zeros(xv.shape, F32)
    alf[...] = jnp.zeros(alf.shape, F32)
    bet[...] = jnp.zeros(bet.shape, F32)
    gam[...] = jnp.ones(gam.shape, F32)
    imdf[...] = jnp.zeros(imdf.shape, F32)
    imdp[...] = jnp.zeros(imdp.shape, F32)
    dpart[...] = jnp.zeros(dpart.shape, F32)

    def first_back(i, carry):
        rows = pl.ds(pl.multiple_of(i * CH, CH), CH)
        turned = t_ref[rows, :].astype(F32).T
        res[0, i] = turned[:HALF]
        res[1, i] = turned[HALF:]
        pltpu.make_async_copy(a_hbm.at[rows, :], a.at[rows, :], a_sem.at[i]).wait()
        got = jnp.dot(turned.astype(BF), a[rows, :], preferred_element_type=F32)

        @pl.when(i == 0)
        def _():
            hacc[0] = got[:HALF]
            hacc[1] = got[HALF:]

        @pl.when(i > 0)
        def _():
            hacc[0] += got[:HALF]
            hacc[1] += got[HALF:]

        return carry

    lax.fori_loop(0, NCH, first_back, 0)
    pl.semaphore_wait(barrier, 127)

    def forward(g):
        def chunk(i, carry):
            rows = pl.ds(pl.multiple_of(i * CH, CH), CH)
            part = None
            for b in range(NY):
                term = lax.dot_general(
                    q[g, b], a[rows, b * LY:(b + 1) * LY], (((1,), (1,)), ((), ())),
                    preferred_element_type=F32)
                part = term if part is None else part + term
            part = part + bet[g][:, :1] * imdp[g, i]
            imdp[g, i] = part
            ps[g, i] = part.astype(BF)
            remote(ps.at[g, i], pr.at[g, i], ex_s.at[g, i], ex_r.at[g, i], across).start()
            return carry

        lax.fori_loop(0, NCH, chunk, 0)

    def back(g, t):
        def chunk(i, delta):
            rows = pl.ds(pl.multiple_of(i * CH, CH), CH)
            res[g, i] = res[g, i] - alf[g][:, :1] * imdf[g, i]
            copy = remote(ps.at[g, i], pr.at[g, i], ex_s.at[g, i], ex_r.at[g, i], across)
            copy.wait_recv()
            copy.wait_send()
            image = ps[g, i].astype(F32) + pr[g, i].astype(F32)
            imdf[g, i] = image
            square = image * image
            for b in range(CH // 128):
                delta = delta + square[:, b * 128:(b + 1) * 128]

            @pl.when(t < 2 * ITERS - 2)
            def _():
                got = jnp.dot(image.astype(BF), a[rows, :], preferred_element_type=F32)

                @pl.when(i == 0)
                def _():
                    hacc[g] = got

                @pl.when(i > 0)
                def _():
                    hacc[g] += got

            return delta

        dpart[g] = lax.fori_loop(0, NCH, chunk, jnp.zeros((HALF, 128), F32))

    def to_owner(g):
        @pl.when(core != g)
        def _():
            for b in range(NY):
                hb[b] = hacc[g, :, b * LY:(b + 1) * LY].astype(BF)
            remote(hb, hd, d2h_s, d2h_r, partner).start()
            remote(dpart.at[g], ddp, d2d_s, d2d_r, partner).start()

        @pl.when(core == g)
        def _():
            big = remote(hb, hd, d2h_s, d2h_r, partner)
            small = remote(dpart.at[g], ddp, d2d_s, d2d_r, partner)
            small.wait_recv()
            delta = jnp.sum(dpart[g] + ddp[...], axis=1, keepdims=True)
            dlt[...] = two_parts(delta, 0).astype(BF)
            big.wait_recv()
            for b in range(NY):
                hs[b] = (hacc[g, :, b * LY:(b + 1) * LY] + hd[b].astype(F32)).astype(BF)
            for j in PLANE:
                y_, z_ = around(j)
                to = dev(xl, y_, z_, core, col)
                rows = pl.ds(pl.multiple_of(z_ * FG, FG), FG)
                remote(hs.at[y_, rows, :], rsh.at[j], rsh_s, rsh_r, to).start()
                remote(dlt.at[rows, :], rsd.at[j], rsd_s, rsd_r, to).start()

    my_rows = pl.ds(pl.multiple_of(z * FG, FG), FG)

    def plane_sum(g, it):
        @pl.when(core == g)
        def _():
            p = lax.rem(it, 2)
            total = hs[y, my_rows, :].astype(F32)
            tile = dlt[my_rows, :].astype(F32)
            big = remote(rsh.at[pl.ds(1, 15)], rsh.at[pl.ds(1, 15)], rsh_s, rsh_r, partner)
            small = remote(rsd.at[pl.ds(1, 15)], rsd.at[pl.ds(1, 15)], rsd_s, rsd_r, partner)
            small.wait_recv()
            big.wait_recv()
            for j in range(1, 16):
                total = total + rsh[j].astype(F32)
                tile = tile + rsd[j].astype(F32)
            xs[p, :, :LY] = total
            xs[p, :, LY:] = tile
            remote(xs.at[p], xr.at[p], x_s.at[p], x_r.at[p], beside).start()
            big.wait_send()
            small.wait_send()

    def update(g, it):
        @pl.when(core == g)
        def _():
            p = lax.rem(it, 2)
            scale = s_ref[y]
            gamma = gam[g, my_rows, :][:, :1]
            beta = bet[g, my_rows, :][:, :1]
            direction = gv[...] + beta * dv[...]
            dv[...] = direction
            copy = remote(xs.at[p], xr.at[p], x_s.at[p], x_r.at[p], beside)
            copy.wait()
            both = xs[p] + xr[p]
            delta = jnp.sum(both[:, LY:], axis=1, keepdims=True)
            alpha = jnp.where(it == 0, -1.0, gamma / jnp.where(it == 0, 1.0, delta))
            grad = gv[...] - alpha * (scale * both[:, :LY])
            gv[...] = grad
            q[g, y, my_rows, :] = (scale * grad).astype(BF)
            square = jnp.sum(grad * grad, axis=1, keepdims=True)
            slot = col * 4 + y
            scal[slot, my_rows, :] = (two_parts(square, 0) + two_parts(alpha, 2)).astype(BF)
            for j in PLANE:
                y_, z_ = around(j)
                to = dev(xl, y_, z_, core, col)
                remote(q.at[g, y, my_rows, :], q.at[g, y, my_rows, :], q_s, q_r, to).start()
                far = dev(xl, y_, z_, core, 1 - col)
                remote(scal.at[slot, my_rows, :], scal.at[slot, my_rows, :], sc_s, sc_r, far).start()
                remote(scal.at[slot, my_rows, :], scal.at[slot, my_rows, :], sc_s, sc_r, to).start()
            far = dev(xl, y, z, core, 1 - col)
            remote(scal.at[slot, my_rows, :], scal.at[slot, my_rows, :], sc_s, sc_r, far).start()
            xv[...] = xv[...] + alpha * direction

    def share(g, it):
        @pl.when(core == g)
        def _():
            big = remote(rsh.at[pl.ds(1, 15)], rsh.at[pl.ds(1, 15)], q_s, q_r, partner)
            small = remote(rsd.at[pl.ds(1, 31)], rsd.at[pl.ds(1, 31)], sc_s, sc_r, partner)
            big.wait_recv()
            remote(q.at[g], q.at[g], qf_s, qf_r, partner).start()
            small.wait_recv()
            tile = scal[0].astype(F32)
            for b in range(1, 8):
                tile = tile + scal[b].astype(F32)
            stile[g] = tile
            remote(stile.at[g], stile.at[g], st_s, st_r, partner).start()
            big.wait_send()
            small.wait_send()

        @pl.when(core != g)
        def _():
            remote(hb, hd, d2h_s, d2h_r, partner).wait_send()
            remote(dpart.at[g], ddp, d2d_s, d2d_r, partner).wait_send()
            remote(stile.at[g], stile.at[g], st_s, st_r, partner).wait_recv()

        tile = stile[g]
        at = lanes(tile.shape)
        new = jnp.sum(jnp.where(at < 2, tile, 0.0), axis=1, keepdims=True)
        alpha = jnp.sum(jnp.where(at < 2, 0.0, tile), axis=1, keepdims=True) * 0.125
        old = gam[g][:, :1]
        beta = jnp.where(it == 0, 0.0, new / jnp.where(it == 0, 1.0, old))
        gam[g] = jnp.broadcast_to(new, (HALF, 128))
        alf[g] = jnp.broadcast_to(alpha, (HALF, 128))
        bet[g] = jnp.broadcast_to(beta, (HALF, 128))

        @pl.when(core != g)
        def _():
            remote(q.at[g], q.at[g], qf_s, qf_r, partner).wait_recv()

        @pl.when(core == g)
        def _():
            remote(q.at[g], q.at[g], qf_s, qf_r, partner).wait_send()
            remote(stile.at[g], stile.at[g], st_s, st_r, partner).wait_send()

    to_owner(0)
    to_owner(1)
    plane_sum(0, 0)
    update(0, 0)
    share(0, 0)

    def half_step(t, carry):
        g = lax.rem(t, 2)
        o = 1 - g
        it = (t + 1) // 2
        forward(g)

        @pl.when(t < 2 * ITERS - 1)
        def _():
            plane_sum(o, it)
            update(o, it)

        back(g, t)

        @pl.when(t < 2 * ITERS - 2)
        def _():
            to_owner(g)

        @pl.when(t < 2 * ITERS - 1)
        def _():
            share(o, it)

        return carry

    lax.fori_loop(0, 2 * ITERS, half_step, 0)

    delta = jnp.concatenate(
        [jnp.sum(dpart[g], axis=1, keepdims=True) for g in range(2)], axis=0)
    fin[...] = jnp.broadcast_to(delta, (FITS, 128)).T[:8]
    copy = remote(fin, fir, f_s, f_r, partner)
    copy.start()

    def turn(i, carry):
        rows = pl.ds(pl.multiple_of(i * CH, CH), CH)
        ro[rows, :] = jnp.concatenate([res[0, i], res[1, i]], axis=0).T
        return carry

    lax.fori_loop(0, NCH, turn, 0)
    copy.wait()
    total = fin[...] + fir[...]
    fsend[...] = total
    fall[chip] = total

    def spread(j, carry):
        xl_ = lax.rem(xl + j // 16, 2)
        y_ = lax.rem(y + lax.rem(j // 4, 4), 4)
        z_ = lax.rem(z + lax.rem(j, 4), 4)
        remote(fsend, fall.at[chip], g_s, g_r, dev(xl_, y_, z_, core, col)).start()
        return carry

    lax.fori_loop(1, 32, spread, 0)

    def turn2(i, carry):
        rows = pl.ds(pl.multiple_of(i * CH, CH), CH)
        imt[rows, :] = jnp.concatenate([imdf[0, i], imdf[1, i]], axis=0).T
        return carry

    lax.fori_loop(0, NCH, turn2, 0)
    gamma_lane = jnp.concatenate([gam[0], gam[1]], axis=0).T[:8]
    everyone = remote(fall.at[pl.ds(0, 31)], fall.at[pl.ds(0, 31)], g_s, g_r, partner)
    everyone.wait_recv()
    total = fall[0]
    for b in range(1, 32):
        total = total + fall[b]
    alpha_lane = gamma_lane / total
    alpha_col = jnp.broadcast_to(alpha_lane[:1], (128, 128)).T
    alf[0] = alpha_col[:HALF]
    alf[1] = alpha_col[HALF:]
    alpha = alf[core, my_rows, :][:, :1]
    beta = bet[core, my_rows, :][:, :1]
    solved = xv[...] + alpha * (gv[...] + beta * dv[...])
    for b in range(FG // 2):
        xpk[b] = solved[2 * b:2 * b + 2, :]
    my_lanes = pl.ds(pl.multiple_of(y * LY, LY), LY)
    for b in range(FG // 2):
        mine = (y == z) & (z == b // 2) & (core == b % 2)

        @pl.when((xl == core) & jnp.logical_not(mine))
        def _():
            remote(xpk.at[b], xo.at[:, my_lanes], o_s.at[b], o_r.at[y],
                   dev(core, z, b // 2, b % 2, col)).start()

        @pl.when((xl == core) & mine)
        def _():
            xo[:, my_lanes] = xpk[b]

    def finish(i, carry):
        rows = pl.ds(pl.multiple_of(i * CH, CH), CH)
        ro[rows, :] = ro[rows, :] - alpha_lane[:1] * imt[rows, :]
        return carry

    lax.fori_loop(0, NCH, finish, 0)
    for b in range(NY):
        @pl.when(jnp.logical_not((xl == core) & (y == z) & (y == b)))
        def _():
            remote(xpk.at[0], xo.at[:, b * LY:(b + 1) * LY], o_s.at[0], o_r.at[b], partner).wait_recv()
    for b in range(FG // 2):
        mine = (y == z) & (z == b // 2) & (core == b % 2)

        @pl.when((xl == core) & jnp.logical_not(mine))
        def _():
            remote(xpk.at[b], xo.at[:, my_lanes], o_s.at[b], o_r.at[0], partner).wait_send()
    everyone.wait_send()


def per_device(design, targets, col_scale):
    vm = pltpu.VMEM
    dma = pltpu.SemaphoreType.DMA
    scratch = [
        vm((M_LOC, P_LOC), BF),
        vm((2, NY, HALF, LY), BF),
        vm((8, HALF, 128), BF),
        vm((2, HALF, 128), F32),
        vm((2, HALF, P_LOC), F32),
        vm((NY, HALF, LY), BF),
        vm((NY, HALF, LY), BF),
        vm((NY, HALF, LY), BF),
        vm((2, HALF, 128), F32),
        vm((HALF, 128), F32),
        vm((HALF, 128), BF),
        vm((16, FG, LY), BF),
        vm((32, FG, 128), BF),
        vm((2, FG, LY + 128), F32),
        vm((2, FG, LY + 128), F32),
        vm((2, NCH, HALF, CH), BF),
        vm((2, NCH, HALF, CH), BF),
        vm((2, NCH, HALF, CH), F32),
        vm((2, NCH, HALF, CH), F32),
        vm((2, NCH, HALF, CH), F32),
        vm((M_LOC, FITS), F32),
        vm((FG, LY), F32),
        vm((FG, LY), F32),
        vm((FG, LY), F32),
        vm((2, HALF, 128), F32),
        vm((2, HALF, 128), F32),
        vm((2, HALF, 128), F32),
        vm((FG // 2, 2, LY), F32),
        vm((8, 128), F32),
        vm((8, 128), F32),
        vm((32, 8, 128), F32),
        vm((8, 128), F32),
        dma((NCH,)),
        dma((2, NCH)), dma((2, NCH)),
        dma(()), dma(()), dma(()), dma(()),
        dma(()), dma(()), dma(()), dma(()),
        dma((2,)), dma((2,)),
        dma(()), dma(()), dma(()), dma(()),
        dma(()), dma(()), dma(()), dma(()),
        dma(()), dma(()), dma(()), dma(()),
        dma((FG // 2,)), dma((NY,)),
    ]
    vmem = pl.BlockSpec(memory_space=pltpu.VMEM)
    xo, ro = pl.pallas_call(
        kernel,
        out_shape=(
            jax.ShapeDtypeStruct((2, P_LOC), F32),
            jax.ShapeDtypeStruct((M_LOC, FITS), F32),
        ),
        in_specs=[pl.BlockSpec(memory_space=pl.ANY), vmem, vmem],
        out_specs=(vmem, vmem),
        scratch_shapes=scratch,
        compiler_params=pltpu.CompilerParams(
            collective_id=0, has_side_effects=True, vmem_limit_bytes=48 * 1024 * 1024),
        name="cg_solve",
    )(design, targets, col_scale.reshape(NY, 1, LY))
    return xo.T, ro


def solution(mesh):
    return jax.shard_map(
        per_device, mesh=mesh,
        in_specs=(P("rows", "cols"), P("rows", None), P("cols")),
        out_specs=(P("cols", "rows"), P("rows", None)),
        check_vma=False,
    )
```

time: 831 us -> 243 us (0.29); the launches traced: 821 us -> 243 us
  blocking collectives: 609 us -> 0 us
  Pallas kernels: 0 us -> 239 us
  matrix products: 101 us -> 0 us
  starting transfers between devices: 30.7 us -> 0 us
  waiting for transfers between devices: 28.1 us -> 0 us
  local copies, waits for them, and re-layouts: 30.7 us -> 3.32 us
  other arithmetic: 19.8 us -> 0 us
    all_to_all x21 -> x0, blocking collectives: 419 us -> none  [the longest x16 280 us: from_everyone(): return lax.all_to_all(copies, axis, split_axis=0, concat_axis=0, tiled=True)]
    pallas_call x0 -> x1, Pallas kernels: none -> 239 us  [per_device(): pl.pallas_call(kernel, out_shape=(jax.ShapeDtypeStruct((2, P_LOC), F32),...]
    psum x30 -> x0, blocking collectives: 190 us -> none  [over_axes(): return functools.reduce(lax.psum, axes, array)]
    dot_general x12 -> x0, matrix products: 101 us -> none  [the longest x6 53.5 us: per_device(): jnp.dot(design, gathered_copies(scaled_dir, ROWS, 0), preferred_element_t...]
    all_to_all x4 -> x0, starting transfers between devices: 30.7 us -> none  [the longest x1 10.9 us: sent_and_summed(): lax.all_to_all(pieces, axis, split_axis=0, concat_axis=0, tiled=True)]
    all_to_all x4 -> x0, waiting for transfers between devices: 28.1 us -> none  [the longest x1 21.7 us: sent_and_summed(): lax.all_to_all(pieces, axis, split_axis=0, concat_axis=0, tiled=True)]
    dot_general x5 -> x0, local copies, waits for them, and re-layouts: 12.8 us -> none  [local_back(): lax.dot_general(design, vectors, (((0,), (0,)), ((), ())), preferred_elem...]
    reduce_sum x30 -> x0, other arithmetic: 12 us -> none  [the longest x6 7.78 us: sent_and_summed(): return arrived.sum(axis=0)]
  transfers between devices with their start and end apart: 4 -> 0, of which waited for: 2 -> 0; matrix products, arithmetic and copies ran while one was open for 2% -> 0% of each run, Pallas kernels for 0% -> 0%
where the time goes in v1:
time: 243 us
  Pallas kernels  239 us (98%)
  local copies, waits for them, and re-layouts  3.32 us (1%)
    pallas_call x1, Pallas kernels, per_device(): pl.pallas_call(kernel, out_shape=(jax.ShapeDtypeStruct((2, P_LOC), F32),...  239 us

profile of v1, /device:TPU:1, one launch (start us, length us, event | category | flops | bytes accessed | tf_op | source)
XLA Modules:
  0.0 243.1 jit_solution(13309455024411992552)
XLA Ops:
  0.6 0.0 copy-start
  0.6 1.0 copy-done
  1.7 0.0 copy-start.1
  1.7 0.7 copy-done.1
  2.4 239.1 %cg_solve.1 = (f32[2,3072]{1,0:T(2,128)S(1)}, f32[2048,128]{1,0:T(8,128)S(1)}) custom-call(bf16[2048,3072]{1,0:T(8,128)(2,1)} %a_hbm.1, bf16[2048,128]{1,0:T(8,128)(2,1)S(1)} %copy-done, f32[4,1,768]{2,1,0:T(1,128)S(1)} %bitcast.3), custom_call_target="tpu_custom_call" | custom-call | tf_op jit(solution)/shard_map/cg_solve/pallas_call | solution.py:435
  241.5 0.6 copy.7
  242.1 1.0 copy.8
Async XLA Ops:
  0.6 1.0 copy-start
  1.7 0.7 copy-start.1

commit v2 on v1

v2 whole, which is shorter than its diff:
```python
import functools

import jax
import jax.numpy as jnp
from jax import lax
from jax.experimental import pallas as pl
from jax.experimental.pallas import tpu as pltpu
from jax.sharding import PartitionSpec as P

ITERS = 6
NX, NY, NZ, NCORE, NCOL = 2, 4, 4, 2, 2
M_LOC, P_LOC, FITS = 2048, 3072, 128
HALF = FITS // 2
FG = HALF // NZ
NBLK = NX * NY
LB = P_LOC // NBLK
CH = 512
NCH = M_LOC // CH
BF, F32 = jnp.bfloat16, jnp.float32
MESH = pl.DeviceIdType.MESH


def wrap_distance(step):
    return min(step, 4 - step)


def far_first(steps, distance):
    return sorted(steps, key=lambda j: -distance(j))


BLOCKS = far_first(range(NBLK), lambda j: j // 4 + wrap_distance(j % 4))
ZS = far_first(range(NZ), wrap_distance)


def rows_and_lanes():
    row = lax.broadcasted_iota(jnp.int32, (FG, 128), 0)
    lane = lax.broadcasted_iota(jnp.int32, (FG, 128), 1)
    return row, lane


def laid_along(column, first):
    row, lane = rows_and_lanes()
    return jnp.sum(jnp.where(lane == row + first, column, 0.0), axis=0, keepdims=True)


def stood_up(line, first):
    row, lane = rows_and_lanes()
    return jnp.sum(jnp.where(lane == row + first, line, 0.0), axis=1, keepdims=True)


def kernel(a_hbm, t_ref, s_ref, xo, ro,
           a, q, scal, stile, hacc, hb, hd, hs, dpart, ddp, dlt, rsh, rsd,
           ps, pr, imdp, imdf, res, imt, gv, dv, xv, gam, alf, bet, xpk, fin, fir, fall, fsend,
           a_sem, ex_s, ex_r, d2h_s, d2h_r, d2d_s, d2d_r, rsh_s, rsh_r, rsd_s, rsd_r,
           q_s, q_r, sc_s, sc_r, qf_s, qf_r, st_s, st_r, f_s, f_r, g_s, g_r, o_s, o_r):
    r = lax.axis_index("rows")
    col = lax.axis_index("cols")
    core = lax.rem(r, 2)
    chip = r // 2
    z = lax.rem(chip, 4)
    y = lax.rem(chip // 4, 4)
    xl = chip // 16

    def dev(xl_, y_, z_, core_, col_):
        return (((xl_ * 4 + y_) * 4 + z_) * 2 + core_, col_)

    def block_at(j):
        return lax.rem(xl + j // 4, 2), lax.rem(y + j % 4, 4)

    def lanes_of(xl_, y_):
        return pl.ds(pl.multiple_of((xl_ * 4 + y_) * LB, LB), LB)

    def rows_of(z_):
        return pl.ds(pl.multiple_of(z_ * FG, FG), FG)

    my_rows = rows_of(z)
    my_lanes = lanes_of(xl, y)
    block = xl * 4 + y
    partner = dev(xl, y, z, 1 - core, col)
    across = dev(xl, y, z, core, 1 - col)

    def remote(src, dst, ss, rs, device):
        return pltpu.make_async_remote_copy(
            src_ref=src, dst_ref=dst, send_sem=ss, recv_sem=rs, device_id=device, device_id_type=MESH)

    for i in range(NCH):
        pltpu.make_async_copy(a_hbm.at[pl.ds(i * CH, CH), :], a.at[pl.ds(i * CH, CH), :], a_sem.at[i]).start()
    barrier = pltpu.get_barrier_semaphore()
    place = ((col * 2 + xl) * 4 + y) * 4 + z

    def greet(j, carry):
        w = lax.rem(place + j, 64)
        other = dev(lax.rem(w // 16, 2), lax.rem(w // 4, 4), lax.rem(w, 4), core, w // 32)
        pl.semaphore_signal(barrier, 1, device_id=other, device_id_type=MESH)
        return carry

    lax.fori_loop(1, 64, greet, 0)
    pl.semaphore_signal(barrier, 1, device_id=partner, device_id_type=MESH)

    def first_back(i, carry):
        rows = pl.ds(pl.multiple_of(i * CH, CH), CH)
        turned = t_ref[rows, :].astype(F32).T
        res[0, i] = turned[:HALF]
        res[1, i] = turned[HALF:]
        pltpu.make_async_copy(a_hbm.at[rows, :], a.at[rows, :], a_sem.at[i]).wait()
        got = jnp.dot(turned.astype(BF), a[rows, :], preferred_element_type=F32)

        @pl.when(i == 0)
        def _():
            hacc[0] = got[:HALF]
            hacc[1] = got[HALF:]

        @pl.when(i > 0)
        def _():
            hacc[0] += got[:HALF]
            hacc[1] += got[HALF:]

        return carry

    lax.fori_loop(0, NCH, first_back, 0)
    gv[...] = jnp.zeros(gv.shape, F32)
    dv[...] = jnp.zeros(dv.shape, F32)
    xv[...] = jnp.zeros(xv.shape, F32)
    alf[...] = jnp.zeros(alf.shape, F32)
    bet[...] = jnp.zeros(bet.shape, F32)
    gam[...] = jnp.ones(gam.shape, F32)
    imdf[...] = jnp.zeros(imdf.shape, F32)
    imdp[...] = jnp.zeros(imdp.shape, F32)
    dpart[...] = jnp.zeros(dpart.shape, F32)
    pl.semaphore_wait(barrier, 64)

    def forward(g):
        def chunk(i, carry):
            rows = pl.ds(pl.multiple_of(i * CH, CH), CH)
            part = lax.dot_general(
                q[g], a[rows, :], (((1,), (1,)), ((), ())), preferred_element_type=F32)
            part = part + bet[g][:, :1] * imdp[g, i]
            imdp[g, i] = part
            ps[g, i] = part.astype(BF)
            remote(ps.at[g, i], pr.at[g, i], ex_s.at[g, i], ex_r.at[g, i], across).start()
            return carry

        lax.fori_loop(0, NCH, chunk, 0)

    def back(g, t):
        def chunk(i, delta):
            rows = pl.ds(pl.multiple_of(i * CH, CH), CH)
            res[g, i] = res[g, i] - alf[g][:, :1] * imdf[g, i]
            copy = remote(ps.at[g, i], pr.at[g, i], ex_s.at[g, i], ex_r.at[g, i], across)
            copy.wait_recv()
            copy.wait_send()
            image = ps[g, i].astype(F32) + pr[g, i].astype(F32)
            imdf[g, i] = image
            square = image * image
            for b in range(CH // 128):
                delta = delta + square[:, b * 128:(b + 1) * 128]

            @pl.when(t < 2 * ITERS - 2)
            def _():
                got = jnp.dot(image.astype(BF), a[rows, :], preferred_element_type=F32)

                @pl.when(i == 0)
                def _():
                    hacc[g] = got

                @pl.when(i > 0)
                def _():
                    hacc[g] += got

            return delta

        dpart[g] = lax.fori_loop(0, NCH, chunk, jnp.zeros((HALF, 128), F32))

    def to_owner(g):
        @pl.when(core != g)
        def _():
            remote(dpart.at[g], ddp, d2d_s, d2d_r, partner).start()
            for j in BLOCKS:
                at = lanes_of(*block_at(j))
                hb[:, at] = hacc[g, :, at].astype(BF)
                remote(hb.at[:, at], hd.at[:, at], d2h_s.at[j], d2h_r.at[j], partner).start()

        @pl.when(core == g)
        def _():
            remote(dpart.at[g], ddp, d2d_s, d2d_r, partner).wait_recv()
            delta = jnp.sum(dpart[g] + ddp[...], axis=1, keepdims=True)
            for b in range(NZ):
                dlt[b] = laid_along(delta[b * FG:(b + 1) * FG], 0)
            for j in BLOCKS:
                xl_, y_ = block_at(j)
                at = lanes_of(xl_, y_)
                remote(hb.at[:, at], hd.at[:, at], d2h_s.at[j], d2h_r.at[j], partner).wait_recv()
                hs[:, at] = (hacc[g, :, at] + hd[:, at].astype(F32)).astype(BF)
                for dz in ZS:
                    if j or dz:
                        z_ = lax.rem(z + dz, 4)
                        to = dev(xl_, y_, z_, core, col)
                        remote(hs.at[rows_of(z_), at], rsh.at[j * 4 + dz], rsh_s, rsh_r, to).start()
                        remote(dlt.at[z_], rsd.at[j * 4 + dz], rsd_s, rsd_r, to).start()

    def update(g, it):
        @pl.when(core == g)
        def _():
            scale = s_ref[block]
            gamma = gam[g, my_rows, :][:, :1]
            beta = bet[g, my_rows, :][:, :1]
            direction = gv[...] + beta * dv[...]
            dv[...] = direction
            big = remote(rsh.at[pl.ds(1, 31)], rsh.at[pl.ds(1, 31)], rsh_s, rsh_r, partner)
            small = remote(rsd.at[pl.ds(1, 31)], rsd.at[pl.ds(1, 31)], rsd_s, rsd_r, partner)
            small.wait_recv()
            line = dlt[z]
            for j in range(1, 32):
                line = line + rsd[j]
            delta = stood_up(line, 0)
            alpha = jnp.where(it == 0, -1.0, gamma / jnp.where(it == 0, 1.0, delta))
            big.wait_recv()
            total = hs[my_rows, my_lanes].astype(F32)
            for j in range(1, 32):
                total = total + rsh[j].astype(F32)
            grad = gv[...] - alpha * (scale * total)
            gv[...] = grad
            q[g, my_rows, my_lanes] = (scale * grad).astype(BF)
            square = jnp.sum(grad * grad, axis=1, keepdims=True)
            slot = (col * NBLK + block) * NZ + z
            scal[slot] = laid_along(square, 0) + laid_along(alpha, FG)
            for j in BLOCKS:
                xl_, y_ = block_at(j)
                back_step = (j // 4) * 4 + (4 - j % 4) % 4
                for dz in ZS:
                    z_ = lax.rem(z + dz, 4)
                    far = dev(xl_, y_, z_, core, 1 - col)
                    remote(scal.at[slot], scal.at[slot], sc_s, sc_r, far).start()
                    if j or dz:
                        to = dev(xl_, y_, z_, core, col)
                        remote(q.at[g, my_rows, my_lanes], q.at[g, my_rows, my_lanes],
                               q_s, q_r.at[back_step], to).start()
                        remote(scal.at[slot], scal.at[slot], sc_s, sc_r, to).start()
            xv[...] = xv[...] + alpha * direction
            big.wait_send()
            small.wait_send()

    def share(g, it):
        @pl.when(core == g)
        def _():
            small = remote(scal.at[pl.ds(0, 63)], scal.at[pl.ds(0, 63)], sc_s, sc_r, partner)
            for j in reversed(BLOCKS):
                count = 64 if j else 48
                got = hd.at[pl.ds(0, count), pl.ds(0, LB)]
                remote(got, got, q_s, q_r.at[j], partner).wait_recv()
                at = lanes_of(*block_at(j))
                remote(q.at[g, :, at], q.at[g, :, at], qf_s.at[j], qf_r.at[j], partner).start()
            small.wait_recv()
            for b in range(NZ):
                line = scal[b]
                for k in range(1, 2 * NBLK):
                    line = line + scal[k * NZ + b]
                gsum = stood_up(line, 0)
                asum = stood_up(line, FG) * (1.0 / (2 * NBLK))
                _, lane = rows_and_lanes()
                stile[g, b * FG:(b + 1) * FG, :] = jnp.where(lane == 0, gsum, asum)
            remote(stile.at[g], stile.at[g], st_s, st_r, partner).start()
            sent = rsh.at[pl.ds(1, 31)]
            remote(sent, sent, q_s, q_r.at[0], partner).wait_send()
            small.wait_send()

        @pl.when(core != g)
        def _():
            for j in BLOCKS:
                at = lanes_of(*block_at(j))
                remote(hb.at[:, at], hd.at[:, at], d2h_s.at[j], d2h_r.at[j], partner).wait_send()
            remote(dpart.at[g], ddp, d2d_s, d2d_r, partner).wait_send()
            remote(stile.at[g], stile.at[g], st_s, st_r, partner).wait_recv()

        tile = stile[g]
        new, alpha = tile[:, :1], tile[:, 1:2]
        old = gam[g][:, :1]
        beta = jnp.where(it == 0, 0.0, new / jnp.where(it == 0, 1.0, old))
        gam[g] = jnp.broadcast_to(new, (HALF, 128))
        alf[g] = jnp.broadcast_to(alpha, (HALF, 128))
        bet[g] = jnp.broadcast_to(beta, (HALF, 128))

        @pl.when(core != g)
        def _():
            for j in BLOCKS:
                at = lanes_of(*block_at(j))
                remote(q.at[g, :, at], q.at[g, :, at], qf_s.at[j], qf_r.at[j], partner).wait_recv()

        @pl.when(core == g)
        def _():
            for j in BLOCKS:
                at = lanes_of(*block_at(j))
                remote(q.at[g, :, at], q.at[g, :, at], qf_s.at[j], qf_r.at[j], partner).wait_send()
            remote(stile.at[g], stile.at[g], st_s, st_r, partner).wait_send()

    to_owner(0)
    to_owner(1)
    update(0, 0)
    share(0, 0)

    def half_step(t, carry):
        g = lax.rem(t, 2)
        o = 1 - g
        it = (t + 1) // 2
        forward(g)

        @pl.when(t < 2 * ITERS - 1)
        def _():
            update(o, it)

        back(g, t)

        @pl.when(t < 2 * ITERS - 2)
        def _():
            to_owner(g)

        @pl.when(t < 2 * ITERS - 1)
        def _():
            share(o, it)

        return carry

    lax.fori_loop(0, 2 * ITERS, half_step, 0)

    delta = jnp.concatenate(
        [jnp.sum(dpart[g], axis=1, keepdims=True) for g in range(2)], axis=0)
    fin[...] = jnp.broadcast_to(delta, (FITS, 128)).T[:8]
    copy = remote(fin, fir, f_s, f_r, partner)
    copy.start()

    def turn(i, carry):
        rows = pl.ds(pl.multiple_of(i * CH, CH), CH)
        ro[rows, :] = jnp.concatenate([res[0, i], res[1, i]], axis=0).T
        return carry

    lax.fori_loop(0, NCH, turn, 0)
    copy.wait()
    total = fin[...] + fir[...]
    fsend[...] = total
    fall[chip] = total

    def spread(j, carry):
        xl_ = lax.rem(xl + j // 16, 2)
        y_ = lax.rem(y + lax.rem(j // 4, 4), 4)
        z_ = lax.rem(z + lax.rem(j, 4), 4)
        remote(fsend, fall.at[chip], g_s, g_r, dev(xl_, y_, z_, core, col)).start()
        return carry

    lax.fori_loop(1, 32, spread, 0)

    def turn2(i, carry):
        rows = pl.ds(pl.multiple_of(i * CH, CH), CH)
        imt[rows, :] = jnp.concatenate([imdf[0, i], imdf[1, i]], axis=0).T
        return carry

    lax.fori_loop(0, NCH, turn2, 0)
    gamma_lane = jnp.concatenate([gam[0], gam[1]], axis=0).T[:8]
    everyone = remote(fall.at[pl.ds(0, 31)], fall.at[pl.ds(0, 31)], g_s, g_r, partner)
    everyone.wait_recv()
    total = fall[0]
    for b in range(1, 32):
        total = total + fall[b]
    alpha_lane = gamma_lane / total
    alpha_col = jnp.broadcast_to(alpha_lane[:1], (128, 128)).T
    alf[0] = alpha_col[:HALF]
    alf[1] = alpha_col[HALF:]
    alpha = alf[core, my_rows, :][:, :1]
    beta = bet[core, my_rows, :][:, :1]
    solved = xv[...] + alpha * (gv[...] + beta * dv[...])
    for b in range(FG // 2):
        xpk[b] = solved[2 * b:2 * b + 2, :]
    for b in range(FG // 2):
        mine = (xl == core) & (y == z) & (z == b // 2) & (core == b % 2)

        @pl.when(jnp.logical_not(mine))
        def _():
            remote(xpk.at[b], xo.at[:, my_lanes], o_s.at[b], o_r.at[block],
                   dev(core, z, b // 2, b % 2, col)).start()

        @pl.when(mine)
        def _():
            xo[:, my_lanes] = xpk[b]

    def finish(i, carry):
        rows = pl.ds(pl.multiple_of(i * CH, CH), CH)
        ro[rows, :] = ro[rows, :] - alpha_lane[:1] * imt[rows, :]
        return carry

    lax.fori_loop(0, NCH, finish, 0)
    for b in range(NBLK):
        @pl.when(jnp.logical_not((xl == core) & (y == z) & (block == b)))
        def _():
            remote(xpk.at[0], xo.at[:, b * LB:(b + 1) * LB], o_s.at[0], o_r.at[b], partner).wait_recv()
    for b in range(FG // 2):
        mine = (xl == core) & (y == z) & (z == b // 2) & (core == b % 2)

        @pl.when(jnp.logical_not(mine))
        def _():
            remote(xpk.at[b], xo.at[:, my_lanes], o_s.at[b], o_r.at[0], partner).wait_send()
    everyone.wait_send()


def per_device(design, targets, col_scale):
    vm = pltpu.VMEM
    dma = pltpu.SemaphoreType.DMA
    scratch = [
        vm((M_LOC, P_LOC), BF),
        vm((2, HALF, P_LOC), BF),
        vm((2 * NBLK * NZ, 1, 128), F32),
        vm((2, HALF, 128), F32),
        vm((2, HALF, P_LOC), F32),
        vm((HALF, P_LOC), BF),
        vm((HALF, P_LOC), BF),
        vm((HALF, P_LOC), BF),
        vm((2, HALF, 128), F32),
        vm((HALF, 128), F32),
        vm((NZ, 1, 128), F32),
        vm((32, FG, LB), BF),
        vm((32, 1, 128), F32),
        vm((2, NCH, HALF, CH), BF),
        vm((2, NCH, HALF, CH), BF),
        vm((2, NCH, HALF, CH), F32),
        vm((2, NCH, HALF, CH), F32),
        vm((2, NCH, HALF, CH), F32),
        vm((M_LOC, FITS), F32),
        vm((FG, LB), F32),
        vm((FG, LB), F32),
        vm((FG, LB), F32),
        vm((2, HALF, 128), F32),
        vm((2, HALF, 128), F32),
        vm((2, HALF, 128), F32),
        vm((FG // 2, 2, LB), F32),
        vm((8, 128), F32),
        vm((8, 128), F32),
        vm((32, 8, 128), F32),
        vm((8, 128), F32),
        dma((NCH,)),
        dma((2, NCH)), dma((2, NCH)),
        dma((NBLK,)), dma((NBLK,)),
        dma(()), dma(()),
        dma(()), dma(()), dma(()), dma(()),
        dma(()), dma((NBLK,)),
        dma(()), dma(()),
        dma((NBLK,)), dma((NBLK,)),
        dma(()), dma(()),
        dma(()), dma(()), dma(()), dma(()),
        dma((FG // 2,)), dma((NBLK,)),
    ]
    vmem = pl.BlockSpec(memory_space=pltpu.VMEM)
    xo, ro = pl.pallas_call(
        kernel,
        out_shape=(
            jax.ShapeDtypeStruct((2, P_LOC), F32),
            jax.ShapeDtypeStruct((M_LOC, FITS), F32),
        ),
        in_specs=[pl.BlockSpec(memory_space=pl.ANY), vmem, vmem],
        out_specs=(vmem, vmem),
        scratch_shapes=scratch,
        compiler_params=pltpu.CompilerParams(
            collective_id=0, has_side_effects=True, vmem_limit_bytes=48 * 1024 * 1024),
        name="cg_solve",
    )(design, targets, col_scale.reshape(NBLK, 1, LB))
    return xo.T, ro


def solution(mesh):
    return jax.shard_map(
        per_device, mesh=mesh,
        in_specs=(P("rows", "cols"), P("rows", None), P("cols")),
        out_specs=(P("cols", "rows"), P("rows", None)),
        check_vma=False,
    )
```

time: 243 us -> 213 us (0.88)
  Pallas kernels: 239 us -> 208 us
    pallas_call x1, Pallas kernels: 239 us -> 208 us  [per_device(): pl.pallas_call(kernel, out_shape=(jax.ShapeDtypeStruct((2, P_LOC), F32),...]
where the time goes in v2:
time: 213 us; the launch traced here: 212 us
  Pallas kernels  208 us (98%)
  local copies, waits for them, and re-layouts  3.32 us (2%)
    pallas_call x1, Pallas kernels, per_device(): pl.pallas_call(kernel, out_shape=(jax.ShapeDtypeStruct((2, P_LOC), F32),...  208 us

profile of v2, /device:TPU:1, one launch (start us, length us, event | category | flops | bytes accessed | tf_op | source)
XLA Modules:
  0.0 212.4 jit_solution(3463077504197458767)
XLA Ops:
  0.6 0.0 copy-start
  0.6 1.0 copy-done
  1.7 0.0 copy-start.1
  1.7 0.7 copy-done.1
  2.4 208.4 %cg_solve.1 = (f32[2,3072]{1,0:T(2,128)S(1)}, f32[2048,128]{1,0:T(8,128)S(1)}) custom-call(bf16[2048,3072]{1,0:T(8,128)(2,1)} %a_hbm.1, bf16[2048,128]{1,0:T(8,128)(2,1)S(1)} %copy-done, f32[8,1,384]{2,1,0:T(1,128)S(1)} %bitcast.3), custom_call_target="tpu_custom_call" | custom-call | tf_op jit(solution)/shard_map/cg_solve/pallas_call | solution.py:450
  210.8 0.6 copy.7
  211.4 1.0 copy.8
Async XLA Ops:
  0.6 1.0 copy-start
  1.7 0.7 copy-start.1

commit v3 on v2

v3 whole, which is shorter than its diff:
```python
import functools

import jax
import jax.numpy as jnp
from jax import lax
from jax.experimental import pallas as pl
from jax.experimental.pallas import tpu as pltpu
from jax.sharding import PartitionSpec as P

ITERS = 6
NX, NY, NZ, NCORE, NCOL = 2, 4, 4, 2, 2
M_LOC, P_LOC, FITS = 2048, 3072, 128
HALF = FITS // 2
FG = HALF // NZ
NBLK = NX * NY
LB = P_LOC // NBLK
CH = 512
NCH = M_LOC // CH
BF, F32 = jnp.bfloat16, jnp.float32
MESH = pl.DeviceIdType.MESH


def wrap_distance(step):
    return min(step, 4 - step)


def far_first(steps, distance):
    return sorted(steps, key=lambda j: -distance(j))


BLOCKS = far_first(range(NBLK), lambda j: j // 4 + wrap_distance(j % 4))
ZS = far_first(range(NZ), wrap_distance)


def across_chunk(tile):
    return jnp.concatenate([tile] * (CH // 128), axis=1)


def rows_and_lanes():
    row = lax.broadcasted_iota(jnp.int32, (FG, 128), 0)
    lane = lax.broadcasted_iota(jnp.int32, (FG, 128), 1)
    return row, lane


def laid_along(column, first):
    row, lane = rows_and_lanes()
    return jnp.sum(jnp.where(lane == row + first, column, 0.0), axis=0, keepdims=True)


def stood_up(line, first):
    row, lane = rows_and_lanes()
    return jnp.sum(jnp.where(lane == row + first, line, 0.0), axis=1, keepdims=True)


def kernel(a_hbm, t_hbm, s_hbm, xo, ro,
           a, at, t_ref, s_ref, q, scal, stile, hacc, hb, hd, hs, dpart, ddp, dlt, rsh, rsd,
           first, ps, pr, imdp, imdf, res, imt, gv, dv, xv, gam, alf, bet, xpk, fall, fsend, xin,
           a_sem, t_sem, s_sem, ex_s, ex_r, d2h_s, d2h_r, d2d_s, d2d_r, rsh_s, rsh_r, rsd_s, rsd_r,
           q_s, q_r, sc_s, sc_r, qf_s, qf_r, st_s, st_r, g_s, g_r, o_s, o_r):
    r = lax.axis_index("rows")
    col = lax.axis_index("cols")
    core = lax.rem(r, 2)
    chip = r // 2
    z = lax.rem(chip, 4)
    y = lax.rem(chip // 4, 4)
    xl = chip // 16

    def dev(xl_, y_, z_, core_, col_):
        return (((xl_ * 4 + y_) * 4 + z_) * 2 + core_, col_)

    def block_at(j):
        return lax.rem(xl + j // 4, 2), lax.rem(y + j % 4, 4)

    def lanes_of(xl_, y_):
        return pl.ds(pl.multiple_of((xl_ * 4 + y_) * LB, LB), LB)

    def rows_of(z_):
        return pl.ds(pl.multiple_of(z_ * FG, FG), FG)

    my_rows = rows_of(z)
    my_lanes = lanes_of(xl, y)
    block = xl * 4 + y
    partner = dev(xl, y, z, 1 - core, col)
    across = dev(xl, y, z, core, 1 - col)

    def remote(src, dst, ss, rs, device):
        return pltpu.make_async_remote_copy(
            src_ref=src, dst_ref=dst, send_sem=ss, recv_sem=rs, device_id=device, device_id_type=MESH)

    pltpu.make_async_copy(t_hbm, t_ref, t_sem).start()
    pltpu.make_async_copy(s_hbm, s_ref, s_sem).start()
    for i in range(NCH):
        pltpu.make_async_copy(a_hbm.at[pl.ds(i * CH, CH), :], a.at[pl.ds(i * CH, CH), :], a_sem.at[i]).start()
    barrier = pltpu.get_barrier_semaphore()
    place = ((col * 2 + xl) * 4 + y) * 4 + z

    def greet(j, carry):
        w = lax.rem(place + j, 64)
        other = dev(lax.rem(w // 16, 2), lax.rem(w // 4, 4), lax.rem(w, 4), core, w // 32)
        pl.semaphore_signal(barrier, 1, device_id=other, device_id_type=MESH)
        return carry

    lax.fori_loop(1, 64, greet, 0)
    pl.semaphore_signal(barrier, 1, device_id=partner, device_id_type=MESH)

    def first_back(i, carry):
        rows = pl.ds(pl.multiple_of(i * CH, CH), CH)
        turned = t_ref[rows, :].astype(F32).T
        res[0, i] = turned[:HALF]
        res[1, i] = turned[HALF:]
        pltpu.make_async_copy(a_hbm.at[rows, :], a.at[rows, :], a_sem.at[i]).wait()
        got = jnp.dot(turned.astype(BF), a[rows, :], preferred_element_type=F32)

        @pl.when(i == 0)
        def _():
            hacc[0] = got[:HALF]
            hacc[1] = got[HALF:]

        @pl.when(i > 0)
        def _():
            hacc[0] += got[:HALF]
            hacc[1] += got[HALF:]

        return carry

    pltpu.make_async_copy(t_hbm, t_ref, t_sem).wait()
    lax.fori_loop(0, NCH, first_back, 0)
    pltpu.make_async_copy(s_hbm, s_ref, s_sem).wait()
    gv[...] = jnp.zeros(gv.shape, F32)
    dv[...] = jnp.zeros(dv.shape, F32)
    xv[...] = jnp.zeros(xv.shape, F32)
    alf[...] = jnp.zeros(alf.shape, F32)
    bet[...] = jnp.zeros(bet.shape, F32)
    gam[...] = jnp.ones(gam.shape, F32)
    imdf[...] = jnp.zeros(imdf.shape, F32)
    imdp[...] = jnp.zeros(imdp.shape, F32)
    dpart[...] = jnp.zeros(dpart.shape, F32)
    pl.semaphore_wait(barrier, 64)

    def turn_design(k, carry):
        eye = (lax.broadcasted_iota(jnp.int32, (256, 256), 0)
               == lax.broadcasted_iota(jnp.int32, (256, 256), 1)).astype(BF)
        part = pl.ds(pl.multiple_of(k * 256, 256), 256)
        for c in range(NCH):
            at[c, part, :] = lax.dot_general(
                eye, a[c * CH:(c + 1) * CH, part], (((1,), (1,)), ((), ())),
                preferred_element_type=F32).astype(BF)
        return carry

    def forward(g, it):
        first[...] = jnp.dot(q[g], at[0], preferred_element_type=F32)
        share_scalars(g, it)
        beta = across_chunk(bet[g])
        for i in range(NCH):
            part = jnp.dot(q[g], at[i], preferred_element_type=F32) if i else first[...]
            part = part + beta * imdp[g, i]
            imdp[g, i] = part
            ps[g, i] = part.astype(BF)
            remote(ps.at[g, i], pr.at[g, i], ex_s.at[g, i], ex_r.at[g, i], across).start()

    def back(g, t):
        @pl.when(core == g)
        def _():
            sent = rsh.at[pl.ds(1, 31)]
            remote(sent, sent, q_s, q_r.at[0], partner).wait_send()
            sent = scal.at[pl.ds(0, 63)]
            remote(sent, sent, sc_s, sc_r, partner).wait_send()
            for j in BLOCKS:
                part = lanes_of(*block_at(j))
                remote(q.at[g, :, part], q.at[g, :, part], qf_s.at[j], qf_r.at[j], partner).wait_send()
            remote(stile.at[g], stile.at[g], st_s, st_r, partner).wait_send()

        hacc[g] = jnp.zeros((HALF, P_LOC), F32)

        def chunk(i, delta):
            rows = pl.ds(pl.multiple_of(i * CH, CH), CH)
            res[g, i] = res[g, i] - across_chunk(alf[g]) * imdf[g, i]
            copy = remote(ps.at[g, i], pr.at[g, i], ex_s.at[g, i], ex_r.at[g, i], across)
            copy.wait_recv()
            copy.wait_send()
            image = ps[g, i].astype(F32) + pr[g, i].astype(F32)
            imdf[g, i] = image
            square = image * image
            for b in range(CH // 128):
                delta = delta + square[:, b * 128:(b + 1) * 128]

            @pl.when(t < 2 * ITERS - 2)
            def _():
                hacc[g] += jnp.dot(image.astype(BF), a[rows, :], preferred_element_type=F32)

            return delta

        dpart[g] = lax.fori_loop(0, NCH, chunk, jnp.zeros((HALF, 128), F32))

    def to_owner(g):
        @pl.when(core != g)
        def _():
            remote(dpart.at[g], ddp, d2d_s, d2d_r, partner).start()
            for j in BLOCKS:
                part = lanes_of(*block_at(j))
                hb[:, part] = hacc[g, :, part].astype(BF)
                remote(hb.at[:, part], hd.at[:, part], d2h_s.at[j], d2h_r.at[j], partner).start()

        @pl.when(core == g)
        def _():
            remote(dpart.at[g], ddp, d2d_s, d2d_r, partner).wait_recv()
            delta = jnp.sum(dpart[g] + ddp[...], axis=1, keepdims=True)
            for b in range(NZ):
                dlt[b] = laid_along(delta[b * FG:(b + 1) * FG], 0)
            for j in BLOCKS:
                xl_, y_ = block_at(j)
                part = lanes_of(xl_, y_)
                remote(hb.at[:, part], hd.at[:, part], d2h_s.at[j], d2h_r.at[j], partner).wait_recv()
                hs[:, part] = (hacc[g, :, part] + hd[:, part].astype(F32)).astype(BF)
                for dz in ZS:
                    if j or dz:
                        z_ = lax.rem(z + dz, 4)
                        to = dev(xl_, y_, z_, core, col)
                        remote(hs.at[rows_of(z_), part], rsh.at[j * 4 + dz], rsh_s, rsh_r, to).start()
            for j in BLOCKS:
                xl_, y_ = block_at(j)
                for dz in ZS:
                    if j or dz:
                        z_ = lax.rem(z + dz, 4)
                        to = dev(xl_, y_, z_, core, col)
                        remote(dlt.at[z_], rsd.at[j * 4 + dz], rsd_s, rsd_r, to).start()

    def update(g, it):
        @pl.when(core == g)
        def _():
            scale = s_ref[block]
            gamma = gam[g, my_rows, :][:, :1]
            beta = bet[g, my_rows, :][:, :1]
            direction = gv[...] + beta * dv[...]
            dv[...] = direction
            big = remote(rsh.at[pl.ds(1, 31)], rsh.at[pl.ds(1, 31)], rsh_s, rsh_r, partner)
            small = remote(rsd.at[pl.ds(1, 31)], rsd.at[pl.ds(1, 31)], rsd_s, rsd_r, partner)
            small.wait_recv()
            line = dlt[z]
            for j in range(1, 32):
                line = line + rsd[j]
            delta = stood_up(line, 0)
            alpha = jnp.where(it == 0, -1.0, gamma / jnp.where(it == 0, 1.0, delta))
            big.wait_recv()
            total = hs[my_rows, my_lanes].astype(F32)
            for j in range(1, 32):
                total = total + rsh[j].astype(F32)
            grad = gv[...] - alpha * (scale * total)
            gv[...] = grad
            q[g, my_rows, my_lanes] = (scale * grad).astype(BF)
            for j in BLOCKS:
                xl_, y_ = block_at(j)
                back_step = (j // 4) * 4 + (4 - j % 4) % 4
                for dz in ZS:
                    if j or dz:
                        to = dev(xl_, y_, lax.rem(z + dz, 4), core, col)
                        remote(q.at[g, my_rows, my_lanes], q.at[g, my_rows, my_lanes],
                               q_s, q_r.at[back_step], to).start()
            square = jnp.sum(grad * grad, axis=1, keepdims=True)
            slot = (col * NBLK + block) * NZ + z
            scal[slot] = laid_along(square, 0) + laid_along(alpha, FG)
            for j in BLOCKS:
                xl_, y_ = block_at(j)
                for dz in ZS:
                    for c in ((1 - col, col) if j or dz else (1 - col,)):
                        to = dev(xl_, y_, lax.rem(z + dz, 4), core, c)
                        remote(scal.at[slot], scal.at[slot], sc_s, sc_r, to).start()
            xv[...] = xv[...] + alpha * direction
            big.wait_send()
            small.wait_send()

    def share(g):
        @pl.when(core == g)
        def _():
            for j in reversed(BLOCKS):
                got = hd.at[pl.ds(0, 64 if j else 48), pl.ds(0, LB)]
                remote(got, got, q_s, q_r.at[j], partner).wait_recv()
                part = lanes_of(*block_at(j))
                remote(q.at[g, :, part], q.at[g, :, part], qf_s.at[j], qf_r.at[j], partner).start()

        @pl.when(core != g)
        def _():
            remote(dpart.at[g], ddp, d2d_s, d2d_r, partner).wait_send()
            for j in BLOCKS:
                part = lanes_of(*block_at(j))
                remote(hb.at[:, part], hd.at[:, part], d2h_s.at[j], d2h_r.at[j], partner).wait_send()
            for j in BLOCKS:
                part = lanes_of(*block_at(j))
                remote(q.at[g, :, part], q.at[g, :, part], qf_s.at[j], qf_r.at[j], partner).wait_recv()

    def share_scalars(g, it):
        @pl.when(core == g)
        def _():
            remote(scal.at[pl.ds(0, 63)], scal.at[pl.ds(0, 63)], sc_s, sc_r, partner).wait_recv()
            for b in range(NZ):
                line = scal[b]
                for k in range(1, 2 * NBLK):
                    line = line + scal[k * NZ + b]
                gsum = stood_up(line, 0)
                asum = stood_up(line, FG) * (1.0 / (2 * NBLK))
                _, lane = rows_and_lanes()
                stile[g, b * FG:(b + 1) * FG, :] = jnp.where(lane == 0, gsum, asum)
            remote(stile.at[g], stile.at[g], st_s, st_r, partner).start()

        @pl.when(core != g)
        def _():
            remote(stile.at[g], stile.at[g], st_s, st_r, partner).wait_recv()

        tile = stile[g]
        new, alpha = tile[:, :1], tile[:, 1:2]
        old = gam[g][:, :1]
        beta = jnp.where(it == 0, 0.0, new / jnp.where(it == 0, 1.0, old))
        gam[g] = jnp.broadcast_to(new, (HALF, 128))
        alf[g] = jnp.broadcast_to(alpha, (HALF, 128))
        bet[g] = jnp.broadcast_to(beta, (HALF, 128))

    to_owner(0)
    lax.fori_loop(0, P_LOC // 256, turn_design, 0)
    update(0, 0)
    to_owner(1)
    share(0)

    def half_step(t, carry):
        g = lax.rem(t, 2)
        o = 1 - g
        it = (t + 1) // 2
        forward(g, t // 2)

        @pl.when(t < 2 * ITERS - 1)
        def _():
            update(o, it)

        back(g, t)

        @pl.when(t < 2 * ITERS - 2)
        def _():
            to_owner(g)

        @pl.when(t < 2 * ITERS - 1)
        def _():
            share(o)

        return carry

    lax.fori_loop(0, 2 * ITERS, half_step, 0)

    delta = jnp.concatenate(
        [jnp.sum(dpart[g], axis=1, keepdims=True) for g in range(2)], axis=0)
    fsend[...] = jnp.broadcast_to(delta, (FITS, 128)).T[:1]
    fall[r] = fsend[...]

    def spread(j, carry):
        remote(fsend, fall.at[r], g_s, g_r, (lax.rem(r + j, 64), col)).start()
        return carry

    lax.fori_loop(1, 64, spread, 0)
    direction = gv[...] + bet[core, my_rows, :][:, :1] * dv[...]
    for b in range(FG // 2):
        xpk[b, :2] = xv[2 * b:2 * b + 2, :]
        xpk[b, 2:] = direction[2 * b:2 * b + 2, :]
    for b in range(FG // 2):
        mine = (xl == core) & (y == z) & (z == b // 2) & (core == b % 2)

        @pl.when(jnp.logical_not(mine))
        def _():
            remote(xpk.at[b], xin.at[block], o_s.at[b], o_r.at[block],
                   dev(core, z, b // 2, b % 2, col)).start()

        @pl.when(mine)
        def _():
            xin[block] = xpk[b]

    def turn(i, carry):
        rows = pl.ds(pl.multiple_of(i * CH, CH), CH)
        ro[rows, :] = jnp.concatenate([res[0, i], res[1, i]], axis=0).T
        return carry

    lax.fori_loop(0, NCH, turn, 0)
    def turn2(i, carry):
        rows = pl.ds(pl.multiple_of(i * CH, CH), CH)
        imt[rows, :] = jnp.concatenate([imdf[0, i], imdf[1, i]], axis=0).T
        return carry

    lax.fori_loop(0, NCH, turn2, 0)
    gamma_lane = jnp.concatenate([gam[0], gam[1]], axis=0).T[:1]
    everyone = remote(fall.at[pl.ds(0, 63)], fall.at[pl.ds(0, 63)], g_s, g_r, partner)
    everyone.wait_recv()
    total = fall[0]
    for b in range(1, 64):
        total = total + fall[b]
    alpha_lane = gamma_lane / total

    def finish(i, carry):
        rows = pl.ds(pl.multiple_of(i * CH, CH), CH)
        ro[rows, :] = ro[rows, :] - alpha_lane * imt[rows, :]
        return carry

    lax.fori_loop(0, NCH, finish, 0)
    mine = lax.broadcasted_iota(jnp.int32, (2, 128), 1) == (
        2 * r + lax.broadcasted_iota(jnp.int32, (2, 128), 0))
    alpha = jnp.sum(jnp.where(mine, alpha_lane, 0.0), axis=1, keepdims=True)
    for b in range(NBLK):
        @pl.when(jnp.logical_not((xl == core) & (y == z) & (block == b)))
        def _():
            remote(xpk.at[0], xin.at[b], o_s.at[0], o_r.at[b], partner).wait_recv()

        xo[:, b * LB:(b + 1) * LB] = xin[b, :2] + alpha * xin[b, 2:]
    for b in range(FG // 2):
        mine = (xl == core) & (y == z) & (z == b // 2) & (core == b % 2)

        @pl.when(jnp.logical_not(mine))
        def _():
            remote(xpk.at[b], xin.at[0], o_s.at[b], o_r.at[0], partner).wait_send()
    everyone.wait_send()


def per_device(design, targets, col_scale):
    vm = pltpu.VMEM
    dma = pltpu.SemaphoreType.DMA
    scratch = [
        vm((M_LOC, P_LOC), BF),
        vm((NCH, P_LOC, CH), BF),
        vm((M_LOC, FITS), BF),
        vm((NBLK, 1, LB), F32),
        vm((2, HALF, P_LOC), BF),
        vm((2 * NBLK * NZ, 1, 128), F32),
        vm((2, HALF, 128), F32),
        vm((2, HALF, P_LOC), F32),
        vm((HALF, P_LOC), BF),
        vm((HALF, P_LOC), BF),
        vm((HALF, P_LOC), BF),
        vm((2, HALF, 128), F32),
        vm((HALF, 128), F32),
        vm((NZ, 1, 128), F32),
        vm((32, FG, LB), BF),
        vm((32, 1, 128), F32),
        vm((HALF, CH), F32),
        vm((2, NCH, HALF, CH), BF),
        vm((2, NCH, HALF, CH), BF),
        vm((2, NCH, HALF, CH), F32),
        vm((2, NCH, HALF, CH), F32),
        vm((2, NCH, HALF, CH), F32),
        vm((M_LOC, FITS), F32),
        vm((FG, LB), F32),
        vm((FG, LB), F32),
        vm((FG, LB), F32),
        vm((2, HALF, 128), F32),
        vm((2, HALF, 128), F32),
        vm((2, HALF, 128), F32),
        vm((FG // 2, 4, LB), F32),
        vm((64, 1, 128), F32),
        vm((1, 128), F32),
        vm((NBLK, 4, LB), F32),
        dma((NCH,)), dma(()), dma(()),
        dma((2, NCH)), dma((2, NCH)),
        dma((NBLK,)), dma((NBLK,)),
        dma(()), dma(()),
        dma(()), dma(()), dma(()), dma(()),
        dma(()), dma((NBLK,)),
        dma(()), dma(()),
        dma((NBLK,)), dma((NBLK,)),
        dma(()), dma(()),
        dma(()), dma(()),
        dma((FG // 2,)), dma((NBLK,)),
    ]
    vmem = pl.BlockSpec(memory_space=pltpu.VMEM)
    xo, ro = pl.pallas_call(
        kernel,
        out_shape=(
            jax.ShapeDtypeStruct((2, P_LOC), F32),
            jax.ShapeDtypeStruct((M_LOC, FITS), F32),
        ),
        in_specs=[pl.BlockSpec(memory_space=pltpu.HBM)] * 3,
        out_specs=(vmem, vmem),
        scratch_shapes=scratch,
        compiler_params=pltpu.CompilerParams(
            collective_id=0, has_side_effects=True, vmem_limit_bytes=50331648),
        name="cg_solve",
    )(
        design,
        pltpu.with_memory_space_constraint(targets, pltpu.HBM),
        pltpu.with_memory_space_constraint(col_scale.reshape(NBLK, 1, LB), pltpu.HBM),
    )
    return xo.T, ro


def solution(mesh):
    return jax.shard_map(
        per_device, mesh=mesh,
        in_specs=(P("rows", "cols"), P("rows", None), P("cols")),
        out_specs=(P("cols", "rows"), P("rows", None)),
        check_vma=False,
    )
```

time: 213 us -> 193 us (0.906)
  Pallas kernels: 208 us -> 191 us
    pallas_call x1, Pallas kernels: 208 us -> 191 us  [per_device(): pl.pallas_call(kernel, out_shape=(jax.ShapeDtypeStruct((2, P_LOC), F32),...]
where the time goes in v3:
time: 193 us
  Pallas kernels  191 us (99%)
    pallas_call x1, Pallas kernels, per_device(): pl.pallas_call(kernel, out_shape=(jax.ShapeDtypeStruct((2, P_LOC), F32),...  191 us

profile of v3, /device:TPU:1, one launch (start us, length us, event | category | flops | bytes accessed | tf_op | source)
XLA Modules:
  0.0 193.1 jit_solution(10444709728603847793)
XLA Ops:
  0.6 190.9 %cg_solve.1 = (f32[2,3072]{1,0:T(2,128)S(1)}, f32[2048,128]{1,0:T(8,128)S(1)}) custom-call(bf16[2048,3072]{1,0:T(8,128)(2,1)} %a_hbm.1, bf16[2048,128]{1,0:T(8,128)(2,1)} %t_hbm.1, f32[8,1,384]{2,1,0:T(1,128)} %bitcast.3), custom_call_target="tpu_custom_call" | custom-call | tf_op jit(solution)/shard_map/cg_solve/pallas_call | solution.py:467
  191.5 0.6 copy.7
  192.2 1.0 copy.8

commit v4 on v3

--- a/solution.py
+++ b/solution.py
@@ -16,6 +16,10 @@
 LB = P_LOC // NBLK
 CH = 512
 NCH = M_LOC // CH
+PARTS = (512, 512, 512, 256, 256)
+STARTS = tuple(sum(PARTS[:k]) for k in range(len(PARTS)))
+AHEAD = 1
+LAST = pl.ds(STARTS[-1], PARTS[-1])
 BF, F32 = jnp.bfloat16, jnp.float32
 MESH = pl.DeviceIdType.MESH
 
@@ -28,12 +32,14 @@
     return sorted(steps, key=lambda j: -distance(j))
 
 
-BLOCKS = far_first(range(NBLK), lambda j: j // 4 + wrap_distance(j % 4))
+CROSSING = far_first(range(4, NBLK), lambda j: wrap_distance(j % 4))
+NEAR = far_first(range(4), wrap_distance)
+BLOCKS = CROSSING + NEAR
 ZS = far_first(range(NZ), wrap_distance)
 
 
-def across_chunk(tile):
-    return jnp.concatenate([tile] * (CH // 128), axis=1)
+def widened(tile, size):
+    return jnp.concatenate([tile] * (size // 128), axis=1)
 
 
 def rows_and_lanes():
@@ -54,7 +60,7 @@
 
 def kernel(a_hbm, t_hbm, s_hbm, xo, ro,
            a, at, t_ref, s_ref, q, scal, stile, hacc, hb, hd, hs, dpart, ddp, dlt, rsh, rsd,
-           first, ps, pr, imdp, imdf, res, imt, gv, dv, xv, gam, alf, bet, xpk, fall, fsend, xin,
+           first, last, ps, pr, imdp, imdf, res, imt, gv, dv, xv, gam, alf, bet, xpk, fall, fsend, xin,
            a_sem, t_sem, s_sem, ex_s, ex_r, d2h_s, d2h_r, d2d_s, d2d_r, rsh_s, rsh_r, rsd_s, rsd_r,
            q_s, q_r, sc_s, sc_r, qf_s, qf_r, st_s, st_r, g_s, g_r, o_s, o_r):
     r = lax.axis_index("rows")
@@ -106,8 +112,8 @@
     def first_back(i, carry):
         rows = pl.ds(pl.multiple_of(i * CH, CH), CH)
         turned = t_ref[rows, :].astype(F32).T
-        res[0, i] = turned[:HALF]
-        res[1, i] = turned[HALF:]
+        res[0, :, rows] = turned[:HALF]
+        res[1, :, rows] = turned[HALF:]
         pltpu.make_async_copy(a_hbm.at[rows, :], a.at[rows, :], a_sem.at[i]).wait()
         got = jnp.dot(turned.astype(BF), a[rows, :], preferred_element_type=F32)
 
@@ -142,21 +148,29 @@
                == lax.broadcasted_iota(jnp.int32, (256, 256), 1)).astype(BF)
         part = pl.ds(pl.multiple_of(k * 256, 256), 256)
         for c in range(NCH):
-            at[c, part, :] = lax.dot_general(
+            at[part, c * CH:(c + 1) * CH] = lax.dot_general(
                 eye, a[c * CH:(c + 1) * CH, part], (((1,), (1,)), ((), ())),
                 preferred_element_type=F32).astype(BF)
         return carry
 
+    def image_copy(g, k):
+        part = pl.ds(STARTS[k], PARTS[k])
+        return remote(ps.at[g, :, part], pr.at[g, :, part], ex_s.at[g, k], ex_r.at[g, k], across)
+
     def forward(g, it):
-        first[...] = jnp.dot(q[g], at[0], preferred_element_type=F32)
+        for c in range(AHEAD):
+            first[c] = jnp.dot(q[g], at[:, c * CH:(c + 1) * CH], preferred_element_type=F32)
         share_scalars(g, it)
-        beta = across_chunk(bet[g])
-        for i in range(NCH):
-            part = jnp.dot(q[g], at[i], preferred_element_type=F32) if i else first[...]
-            part = part + beta * imdp[g, i]
-            imdp[g, i] = part
-            ps[g, i] = part.astype(BF)
-            remote(ps.at[g, i], pr.at[g, i], ex_s.at[g, i], ex_r.at[g, i], across).start()
+        beta = widened(bet[g], CH)
+        for c in range(NCH):
+            part = pl.ds(c * CH, CH)
+            value = first[c] if c < AHEAD else jnp.dot(q[g], at[:, part], preferred_element_type=F32)
+            value = value + beta * imdp[g, :, part]
+            imdp[g, :, part] = value
+            ps[g, :, part] = value.astype(BF)
+            for k, start in enumerate(STARTS):
+                if start // CH == c:
+                    image_copy(g, k).start()
 
     def back(g, t):
         @pl.when(core == g)
@@ -172,34 +186,38 @@
 
         hacc[g] = jnp.zeros((HALF, P_LOC), F32)
 
-        def chunk(i, delta):
-            rows = pl.ds(pl.multiple_of(i * CH, CH), CH)
-            res[g, i] = res[g, i] - across_chunk(alf[g]) * imdf[g, i]
-            copy = remote(ps.at[g, i], pr.at[g, i], ex_s.at[g, i], ex_r.at[g, i], across)
+        delta = jnp.zeros((HALF, 128), F32)
+        for k, (start, size) in enumerate(zip(STARTS, PARTS)):
+            part = pl.ds(start, size)
+            res[g, :, part] = res[g, :, part] - widened(alf[g], size) * imdf[g, :, part]
+            copy = image_copy(g, k)
             copy.wait_recv()
             copy.wait_send()
-            image = ps[g, i].astype(F32) + pr[g, i].astype(F32)
-            imdf[g, i] = image
+            image = ps[g, :, part].astype(F32) + pr[g, :, part].astype(F32)
+            imdf[g, :, part] = image
             square = image * image
-            for b in range(CH // 128):
+            for b in range(size // 128):
                 delta = delta + square[:, b * 128:(b + 1) * 128]
-
-            @pl.when(t < 2 * ITERS - 2)
-            def _():
-                hacc[g] += jnp.dot(image.astype(BF), a[rows, :], preferred_element_type=F32)
-
-            return delta
-
-        dpart[g] = lax.fori_loop(0, NCH, chunk, jnp.zeros((HALF, 128), F32))
-
-    def to_owner(g):
+            if k < len(PARTS) - 1:
+                @pl.when(t < 2 * ITERS - 2)
+                def _():
+                    hacc[g] += jnp.dot(image.astype(BF), a[part, :], preferred_element_type=F32)
+            else:
+                last[...] = image.astype(BF)
+        dpart[g] = delta
+
+    def to_owner(g, start=False):
         @pl.when(core != g)
         def _():
             remote(dpart.at[g], ddp, d2d_s, d2d_r, partner).start()
-            for j in BLOCKS:
-                part = lanes_of(*block_at(j))
-                hb[:, part] = hacc[g, :, part].astype(BF)
-                remote(hb.at[:, part], hd.at[:, part], d2h_s.at[j], d2h_r.at[j], partner).start()
+            for steps, half in ((CROSSING, 1 - xl), (NEAR, xl)):
+                if not start:
+                    part = pl.ds(pl.multiple_of(half * (P_LOC // 2), P_LOC // 2), P_LOC // 2)
+                    hacc[g, :, part] += jnp.dot(last[...], a[LAST, part], preferred_element_type=F32)
+                for j in steps:
+                    part = lanes_of(*block_at(j))
+                    hb[:, part] = hacc[g, :, part].astype(BF)
+                    remote(hb.at[:, part], hd.at[:, part], d2h_s.at[j], d2h_r.at[j], partner).start()
 
         @pl.when(core == g)
         def _():
@@ -207,6 +225,15 @@
             delta = jnp.sum(dpart[g] + ddp[...], axis=1, keepdims=True)
             for b in range(NZ):
                 dlt[b] = laid_along(delta[b * FG:(b + 1) * FG], 0)
+            for j in BLOCKS:
+                xl_, y_ = block_at(j)
+                for dz in ZS:
+                    if j or dz:
+                        z_ = lax.rem(z + dz, 4)
+                        to = dev(xl_, y_, z_, core, col)
+                        remote(dlt.at[z_], rsd.at[j * 4 + dz], rsd_s, rsd_r, to).start()
+            if not start:
+                hacc[g] += jnp.dot(last[...], a[LAST, :], preferred_element_type=F32)
             for j in BLOCKS:
                 xl_, y_ = block_at(j)
                 part = lanes_of(xl_, y_)
@@ -217,13 +244,6 @@
                         z_ = lax.rem(z + dz, 4)
                         to = dev(xl_, y_, z_, core, col)
                         remote(hs.at[rows_of(z_), part], rsh.at[j * 4 + dz], rsh_s, rsh_r, to).start()
-            for j in BLOCKS:
-                xl_, y_ = block_at(j)
-                for dz in ZS:
-                    if j or dz:
-                        z_ = lax.rem(z + dz, 4)
-                        to = dev(xl_, y_, z_, core, col)
-                        remote(dlt.at[z_], rsd.at[j * 4 + dz], rsd_s, rsd_r, to).start()
 
     def update(g, it):
         @pl.when(core == g)
@@ -248,23 +268,31 @@
             grad = gv[...] - alpha * (scale * total)
             gv[...] = grad
             q[g, my_rows, my_lanes] = (scale * grad).astype(BF)
-            for j in BLOCKS:
-                xl_, y_ = block_at(j)
-                back_step = (j // 4) * 4 + (4 - j % 4) % 4
-                for dz in ZS:
-                    if j or dz:
-                        to = dev(xl_, y_, lax.rem(z + dz, 4), core, col)
-                        remote(q.at[g, my_rows, my_lanes], q.at[g, my_rows, my_lanes],
-                               q_s, q_r.at[back_step], to).start()
+            slot = (col * NBLK + block) * NZ + z
+
+            def send_scalars(steps, c):
+                for j in steps:
+                    for dz in ZS:
+                        if j or dz or c is not col:
+                            to = dev(*block_at(j), lax.rem(z + dz, 4), core, c)
+                            remote(scal.at[slot], scal.at[slot], sc_s, sc_r, to).start()
+
+            def send_q(steps):
+                for j in steps:
+                    back_step = (j // 4) * 4 + (4 - j % 4) % 4
+                    for dz in ZS:
+                        if j or dz:
+                            to = dev(*block_at(j), lax.rem(z + dz, 4), core, col)
+                            remote(q.at[g, my_rows, my_lanes], q.at[g, my_rows, my_lanes],
+                                   q_s, q_r.at[back_step], to).start()
+
+            send_q(NEAR)
             square = jnp.sum(grad * grad, axis=1, keepdims=True)
-            slot = (col * NBLK + block) * NZ + z
             scal[slot] = laid_along(square, 0) + laid_along(alpha, FG)
-            for j in BLOCKS:
-                xl_, y_ = block_at(j)
-                for dz in ZS:
-                    for c in ((1 - col, col) if j or dz else (1 - col,)):
-                        to = dev(xl_, y_, lax.rem(z + dz, 4), core, c)
-                        remote(scal.at[slot], scal.at[slot], sc_s, sc_r, to).start()
+            send_scalars(BLOCKS, 1 - col)
+            send_scalars(CROSSING, col)
+            send_q(CROSSING)
+            send_scalars(NEAR, col)
             xv[...] = xv[...] + alpha * direction
             big.wait_send()
             small.wait_send()
@@ -272,7 +300,7 @@
     def share(g):
         @pl.when(core == g)
         def _():
-            for j in reversed(BLOCKS):
+            for j in NEAR[::-1] + CROSSING:
                 got = hd.at[pl.ds(0, 64 if j else 48), pl.ds(0, LB)]
                 remote(got, got, q_s, q_r.at[j], partner).wait_recv()
                 part = lanes_of(*block_at(j))
@@ -314,10 +342,10 @@
         alf[g] = jnp.broadcast_to(alpha, (HALF, 128))
         bet[g] = jnp.broadcast_to(beta, (HALF, 128))
 
-    to_owner(0)
+    to_owner(0, True)
     lax.fori_loop(0, P_LOC // 256, turn_design, 0)
     update(0, 0)
-    to_owner(1)
+    to_owner(1, True)
     share(0)
 
     def half_step(t, carry):
@@ -372,13 +400,13 @@
 
     def turn(i, carry):
         rows = pl.ds(pl.multiple_of(i * CH, CH), CH)
-        ro[rows, :] = jnp.concatenate([res[0, i], res[1, i]], axis=0).T
+        ro[rows, :] = jnp.concatenate([res[0, :, rows], res[1, :, rows]], axis=0).T
         return carry
 
     lax.fori_loop(0, NCH, turn, 0)
     def turn2(i, carry):
         rows = pl.ds(pl.multiple_of(i * CH, CH), CH)
-        imt[rows, :] = jnp.concatenate([imdf[0, i], imdf[1, i]], axis=0).T
+        imt[rows, :] = jnp.concatenate([imdf[0, :, rows], imdf[1, :, rows]], axis=0).T
         return carry
 
     lax.fori_loop(0, NCH, turn2, 0)
@@ -419,7 +447,7 @@
     dma = pltpu.SemaphoreType.DMA
     scratch = [
         vm((M_LOC, P_LOC), BF),
-        vm((NCH, P_LOC, CH), BF),
+        vm((P_LOC, M_LOC), BF),
         vm((M_LOC, FITS), BF),
         vm((NBLK, 1, LB), F32),
         vm((2, HALF, P_LOC), BF),
@@ -434,12 +462,13 @@
         vm((NZ, 1, 128), F32),
         vm((32, FG, LB), BF),
         vm((32, 1, 128), F32),
-        vm((HALF, CH), F32),
-        vm((2, NCH, HALF, CH), BF),
-        vm((2, NCH, HALF, CH), BF),
-        vm((2, NCH, HALF, CH), F32),
-        vm((2, NCH, HALF, CH), F32),
-        vm((2, NCH, HALF, CH), F32),
+        vm((AHEAD, HALF, CH), F32),
+        vm((HALF, PARTS[-1]), BF),
+        vm((2, HALF, M_LOC), BF),
+        vm((2, HALF, M_LOC), BF),
+        vm((2, HALF, M_LOC), F32),
+        vm((2, HALF, M_LOC), F32),
+        vm((2, HALF, M_LOC), F32),
         vm((M_LOC, FITS), F32),
         vm((FG, LB), F32),
         vm((FG, LB), F32),
@@ -452,7 +481,7 @@
         vm((1, 128), F32),
         vm((NBLK, 4, LB), F32),
         dma((NCH,)), dma(()), dma(()),
-        dma((2, NCH)), dma((2, NCH)),
+        dma((2, len(PARTS))), dma((2, len(PARTS))),
         dma((NBLK,)), dma((NBLK,)),
         dma(()), dma(()),
         dma(()), dma(()), dma(()), dma(()),

time: 193 us -> 187 us (0.969)
  Pallas kernels: 191 us -> 185 us
    pallas_call x1, Pallas kernels: 191 us -> 185 us  [per_device(): pl.pallas_call(kernel, out_shape=(jax.ShapeDtypeStruct((2, P_LOC), F32),...]
where the time goes in v4:
time: 187 us
  Pallas kernels  185 us (99%)
    pallas_call x1, Pallas kernels, per_device(): pl.pallas_call(kernel, out_shape=(jax.ShapeDtypeStruct((2, P_LOC), F32),...  185 us

profile of v4, /device:TPU:1, one launch (start us, length us, event | category | flops | bytes accessed | tf_op | source)
XLA Modules:
  0.0 187.2 jit_solution(10751656678915348762)
XLA Ops:
  0.6 184.9 %cg_solve.1 = (f32[2,3072]{1,0:T(2,128)S(1)}, f32[2048,128]{1,0:T(8,128)S(1)}) custom-call(bf16[2048,3072]{1,0:T(8,128)(2,1)} %a_hbm.1, bf16[2048,128]{1,0:T(8,128)(2,1)} %t_hbm.1, f32[8,1,384]{2,1,0:T(1,128)} %bitcast.3), custom_call_target="tpu_custom_call" | custom-call | tf_op jit(solution)/shard_map/cg_solve/pallas_call | solution.py:496
  185.6 0.6 copy.7
  186.2 1.0 copy.8

commit v5 on v4

--- a/solution.py
+++ b/solution.py
@@ -18,6 +18,7 @@
 NCH = M_LOC // CH
 PARTS = (512, 512, 512, 256, 256)
 STARTS = tuple(sum(PARTS[:k]) for k in range(len(PARTS)))
+PROMPT = 3
 AHEAD = 1
 LAST = pl.ds(STARTS[-1], PARTS[-1])
 BF, F32 = jnp.bfloat16, jnp.float32
@@ -169,10 +170,16 @@
             imdp[g, :, part] = value
             ps[g, :, part] = value.astype(BF)
             for k, start in enumerate(STARTS):
-                if start // CH == c:
+                if start // CH != c:
+                    continue
+                if k < PROMPT:
                     image_copy(g, k).start()
-
-    def back(g, t):
+                else:
+                    @pl.when((core != g) | (it == ITERS - 1))
+                    def _():
+                        image_copy(g, k).start()
+
+    def before_back(g):
         @pl.when(core == g)
         def _():
             sent = rsh.at[pl.ds(1, 31)]
@@ -185,13 +192,19 @@
             remote(stile.at[g], stile.at[g], st_s, st_r, partner).wait_send()
 
         hacc[g] = jnp.zeros((HALF, P_LOC), F32)
-
+        res[g] = res[g] - widened(alf[g], M_LOC) * imdf[g]
+
+    def back(g, t):
         delta = jnp.zeros((HALF, 128), F32)
         for k, (start, size) in enumerate(zip(STARTS, PARTS)):
             part = pl.ds(start, size)
-            res[g, :, part] = res[g, :, part] - widened(alf[g], size) * imdf[g, :, part]
             copy = image_copy(g, k)
             copy.wait_recv()
+            if k == 0:
+                @pl.when((core == g) & (t < 2 * ITERS - 2))
+                def _():
+                    for late in range(PROMPT, len(PARTS)):
+                        image_copy(g, late).start()
             copy.wait_send()
             image = ps[g, :, part].astype(F32) + pr[g, :, part].astype(F32)
             imdf[g, :, part] = image
@@ -354,9 +367,17 @@
         it = (t + 1) // 2
         forward(g, t // 2)
 
+        @pl.when(g == 1)
+        def _():
+            before_back(g)
+
         @pl.when(t < 2 * ITERS - 1)
         def _():
             update(o, it)
+
+        @pl.when(g == 0)
+        def _():
+            before_back(g)
 
         back(g, t)
 
@@ -377,11 +398,12 @@
     fsend[...] = jnp.broadcast_to(delta, (FITS, 128)).T[:1]
     fall[r] = fsend[...]
 
-    def spread(j, carry):
-        remote(fsend, fall.at[r], g_s, g_r, (lax.rem(r + j, 64), col)).start()
-        return carry
-
-    lax.fori_loop(1, 64, spread, 0)
+    for j in BLOCKS:
+        for dz in ZS:
+            for c in (1 - core, core):
+                if j or dz or c is not core:
+                    to = dev(*block_at(j), lax.rem(z + dz, 4), c, col)
+                    remote(fsend, fall.at[r], g_s, g_r, to).start()
     direction = gv[...] + bet[core, my_rows, :][:, :1] * dv[...]
     for b in range(FG // 2):
         xpk[b, :2] = xv[2 * b:2 * b + 2, :]

time: 187 us -> 186 us (level)
  no operation moved by 1% of the time
where the time goes in v5:
time: 186 us
  Pallas kernels  184 us (99%)
    pallas_call x1, Pallas kernels, per_device(): pl.pallas_call(kernel, out_shape=(jax.ShapeDtypeStruct((2, P_LOC), F32),...  184 us

profile of v5, /device:TPU:1, one launch (start us, length us, event | category | flops | bytes accessed | tf_op | source)
XLA Modules:
  0.0 185.9 jit_solution(4599501863891834369)
XLA Ops:
  0.6 183.7 %cg_solve.1 = (f32[2,3072]{1,0:T(2,128)S(1)}, f32[2048,128]{1,0:T(8,128)S(1)}) custom-call(bf16[2048,3072]{1,0:T(8,128)(2,1)} %a_hbm.1, bf16[2048,128]{1,0:T(8,128)(2,1)} %t_hbm.1, f32[8,1,384]{2,1,0:T(1,128)} %bitcast.3), custom_call_target="tpu_custom_call" | custom-call | tf_op jit(solution)/shard_map/cg_solve/pallas_call | solution.py:518
  184.3 0.6 copy.7
  184.9 1.0 copy.8
